TPU v7x, 32 devices: a whole 2x2x4 slice. The times are simulated.
32 devices in a mesh: robot: 8 (over z, x), sub: 4 (over y, core).
Axes of the slice: x: 2, y: 2, z: 4, core: 2. Of those that a mesh axis runs over, the one named last changes fastest.
Arguments:
- landmark_copies: float32 [8, 4, 3, 512], P('robot', 'sub'), may hold values from -6 to 6
- dual_copies: float32 [8, 4, 3, 512], P('robot', 'sub'), may hold values from -4 to 4
- visibility: int32 [8, 4, 512], P('robot', 'sub'), may hold values from 0 to 511
- block_counts: int32 [8, 4, 8], P('robot', 'sub'), may hold values from 1 to 64, as said below
- consensus_old: float32 [8, 4, 3, 512], P('robot', 'sub'), may hold values from -6 to 6
- poses: float32 [8, 4, 6, 1024], P('robot', 'sub'), may hold values from -6 to 6
- inverse_blocks: float32 [8, 4, 36, 1024], P('robot', 'sub'), may hold values from -1.8 to 1.8
- jacobians: float32 [8, 4, 18, 4096], P('robot', 'sub'), may hold values from -3 to 3
- measurements: float32 [8, 4, 3, 4096], P('robot', 'sub'), may hold values from -6 to 6
- obs_pose: int32 [8, 4, 4096], P('robot', 'sub'), may hold values from 0 to 1023
- obs_slot: int32 [8, 4, 4096], P('robot', 'sub'), may hold values from 0 to 511, as said below
- edge_to: int32 [8, 4, 1024], P('robot', 'sub'), may hold values from 0 to 4095
- edge_offset: float32 [8, 4, 6, 1024], P('robot', 'sub'), may hold values from -3 to 3
Outputs:
- refined_poses: float32 [8, 4, 6, 1024], P('robot', 'sub')
- consensus: float32 [8, 4, 3, 512], P('robot', 'sub')
- dual_new: float32 [8, 4, 3, 512], P('robot', 'sub')
- residual_norms: float32 [2], replicated
Inputs may be any that keep to these rules, and one draw needn't show every extreme that they name: block_counts[r,s,d] counts the live slots at the head of block d; for every sub index some robot receives full blocks from every robot, which robot varies with the draw. `obs_slot`: each observation names a live slot of its own device.
All inputs are finite; a program needn't handle non-finite values.
Results may differ from a plain program's by a relative error of at most 0.0001.
Values sent between devices are 32-bit elements; how exact they have to be, the bound alone decides.
No kernel may reach another device: no remote copies, remote signals or barrier semaphores. Data moves between devices by JAX's collectives and lax.ppermute only.
A program may use at most 64 MiB of HBM per device.

v0:
```python
import jax
import jax.numpy as jnp
from jax import lax
from jax.sharding import PartitionSpec as P

penalty = 2.0


def body(
    landmark_copies,
    dual_copies,
    visibility,
    block_counts,
    consensus_old,
    poses,
    inverse_blocks,
    jacobians,
    measurements,
    obs_pose,
    obs_slot,
    edge_to,
    edge_offset,
):
    copies = landmark_copies[0, 0]
    duals = dual_copies[0, 0]
    slot_ids = visibility[0]
    counts = block_counts[0, 0]
    old_estimate = consensus_old[0, 0]
    robots = lax.axis_size("robot")
    slot_count = copies.shape[1]
    block_size = slot_count // robots
    owned = old_estimate.shape[1]
    live_mask = (
        (jnp.arange(block_size)[None, :] < counts[:, None]).reshape(slot_count).astype(jnp.float32)
    )
    outgoing = jnp.concatenate([(copies + duals) * live_mask[None, :], live_mask[None, :]], axis=0)
    received, received_ids = (
        lax.all_to_all(outgoing, "robot", split_axis=1, concat_axis=1, tiled=True),
        lax.all_to_all(slot_ids, "robot", split_axis=1, concat_axis=1, tiled=True),
    )
    owner_ids = received_ids[0]
    totals = jax.vmap(lambda entries: jax.ops.segment_sum(entries, owner_ids, num_segments=owned))(
        received
    )
    consensus = (old_estimate + totals[:3]) / (1.0 + totals[3:4])
    returning = consensus[:, owner_ids]
    back = lax.all_to_all(returning, "robot", split_axis=1, concat_axis=1, tiled=True)
    differ = (copies - back) * live_mask[None, :]
    dual_new = duals + differ
    primal = jnp.sum(differ * differ)
    change = consensus - old_estimate
    dualsum = penalty * penalty * jnp.sum(totals[3:4] * change * change)
    primal_all, dual_all = lax.psum((primal, dualsum), ("robot", "sub"))
    landmark_total = owned * robots * lax.axis_size("sub")
    residual_norms = jnp.sqrt(jnp.stack([primal_all, dual_all]) / landmark_total)
    pose_block = poses[0, 0]
    pose_count = pose_block.shape[1]
    robot_all = lax.all_gather(pose_block, "sub", axis=1, tiled=True)
    pose_far = robot_all[:, edge_to[0, 0]]
    copies_at = copies[:, obs_slot[0, 0]]
    error = measurements[0, 0] - copies_at
    jac_rows = jacobians[0, 0].reshape(3, 6, error.shape[1])
    pull = jnp.sum(jac_rows * error[:, None, :], axis=0)
    pose_ids = obs_pose[0, 0]
    grad_obs = jax.vmap(
        lambda entries: jax.ops.segment_sum(entries, pose_ids, num_segments=pose_count)
    )(pull)
    grad = grad_obs + pose_far - pose_block - edge_offset[0, 0]
    inverse = inverse_blocks[0, 0].reshape(6, 6, pose_count)
    delta = jnp.sum(inverse * grad[None, :, :], axis=1)
    refined = pose_block + delta
    return (refined[None, None], consensus[None, None], dual_new[None, None], residual_norms)


def solution(mesh):
    return jax.shard_map(
        body,
        mesh=mesh,
        in_specs=(
            P("robot", "sub", None, None),
            P("robot", "sub", None, None),
            P("robot", "sub", None),
            P("robot", "sub", None),
            P("robot", "sub", None, None),
            P("robot", "sub", None, None),
            P("robot", "sub", None, None),
            P("robot", "sub", None, None),
            P("robot", "sub", None, None),
            P("robot", "sub", None),
            P("robot", "sub", None),
            P("robot", "sub", None),
            P("robot", "sub", None, None),
        ),
        out_specs=(
            P("robot", "sub", None, None),
            P("robot", "sub", None, None),
            P("robot", "sub", None, None),
            P(),
        ),
        check_vma=False,
    )
```

profile of v0, /device:TPU:0, one launch (start us, length us, event | category | flops | bytes accessed | tf_op | source)
XLA Modules:
  0.0 154.9 jit_solution(5562532823633209940)
XLA Ops:
  0.6 0.5 broadcast.115
  1.1 1.3 reduce.16
  2.5 0.7 all_to_all.22
  3.2 7.3 %all-to-all-start = ((s32[1,8,64]{2,0,1:T(1,128)}), s32[1,8,64]{2,0,1:T(1,128)S(1)}, u32[]{:S(2)}, u32[]{:S(2)}) async-start(s32[1,8,64]{2,0,1:T(1,128)} %all_to_all.22), calls=%async_computation | async-start | bytes 8192 | tf_op jit(solution)/shard_map/all_to_all | solution.py:39
  10.4 0.7 fusion.8
  11.2 0.7 fusion.9
  11.9 0.8 copy.53
  12.7 0.7 add_reduce_fusion.1
  13.5 0.1 add.79
  13.6 0.7 compare_select_fusion
  14.3 1.4 copy.52
  15.7 14.1 %gather_fusion.1 = f32[4096,3]{1,0:T(8,128)} fusion(f32[3,512]{0,1:T(8,128)S(1)} %bitcast.54, s32[4096]{0:T(1024)S(1)} %broadcast_clamp_fusion), kind=kCustom, calls=%fused_computation.1 | custom fusion | bytes 114688 | tf_op jit(solution)/shard_map/gather | solution.py:60
  29.8 3.2 %bitcast_subtract_fusion = f32[3,4096]{0,1:T(8,128)} fusion(f32[4096,3]{1,0:T(8,128)} %gather_fusion.1, f32[1,1,3,4096]{2,3,1,0:T(8,128)S(1)} %copy.52), kind=kLoop, calls=%fused_computation.5 | loop fusion | flops 12288 | bytes 147456 | tf_op jit(solution)/shard_map/sub | solution.py:61
  33.0 2.3 %copy.54 = f32[3,4096]{1,0:T(4,128)S(1)} copy(f32[3,4096]{0,1:T(8,128)} %bitcast_subtract_fusion) | data formatting | bytes 98304 | tf_op jit(solution)/shard_map/sub | solution.py:61
  35.2 0.7 reduce.1
  36.0 0.1 multiply_reduce_fusion
  36.1 2.0 %copy.55 = f32[4096,6]{1,0:T(8,128)} copy(f32[4096,6]{0,1:T(8,128)S(1)} %bitcast.57) | data formatting | bytes 196608 | tf_op jit(solution)/shard_map/reduce_sum | solution.py:63
  38.1 0.2 copy.51
  38.3 15.8 %all-gather = f32[1,1,6,4096]{2,3,1,0:T(8,128)S(1)} all-gather(f32[1,1,6,1024]{2,3,1,0:T(8,128)S(1)} %copy.51), channel_id=2, replica_groups=mesh['robot'=8,'sub'=4] {'sub'}, dimensions={3}, use_global_device_ids=true | all-gather | bytes 122880 | tf_op jit(solution)/shard_map/all_gather | solution.py:58
  54.1 1.0 copy.57
  55.1 2.8 %gather_fusion = f32[1024,6]{1,0:T(8,128)S(1)} fusion(f32[6,4096]{0,1:T(8,128)S(1)} %bitcast.55, s32[1024]{0:T(1024)S(1)} %broadcast_clamp_fusion.1), kind=kCustom, calls=%fused_computation | custom fusion | bytes 53248 | tf_op jit(solution)/shard_map/gather | solution.py:59
  58.0 0.0 copy-start.2
  58.0 22.9 %scatter_fusion = f32[6,1024]{0,1:T(8,128)S(1)} fusion(f32[6,1024]{0,1:T(8,128)S(1)} %bitcast.53, s32[4096]{0:T(1024)S(1)} %bitcast.67, f32[4096,6]{1,0:T(8,128)} %copy.55), kind=kCustom, calls=%fused_computation.3 | custom fusion | flops 24576 | bytes 311296 | tf_op jit(solution)/shard_map/vmap()/scatter-add | solution.py:66
  80.9 0.0 copy-done
  80.9 0.0 copy-start.8
  80.9 0.1 bitcast_subtract_fusion.1
  81.0 0.2 copy.58
  81.2 0.4 reduce
  81.6 0.0 copy-start.4
  81.6 0.0 copy-start.6
  81.6 0.1 multiply_reduce_fusion.1
  81.7 0.7 reshape.262
  82.4 0.1 copy.59
  82.6 0.0 all-to-all-done
  82.6 6.0 %all-to-all-start.1 = ((f32[8,1,256]{2,1,0:T(1,128)}), f32[8,1,256]{2,1,0:T(1,128)S(1)}, u32[]{:S(2)}, u32[]{:S(2)}) async-start(f32[8,1,256]{2,1,0:T(1,128)} %reshape.262), calls=%async_computation.1 | async-start | bytes 16384 | tf_op jit(solution)/shard_map/all_to_all | solution.py:38
  88.6 0.1 broadcast_in_dim_squeeze.8
  88.7 0.7 reduce.17
  89.3 0.1 reshape.227
  89.4 5.7 %all-to-all-done.1 = f32[8,1,256]{2,1,0:T(1,128)S(1)} async-done(((f32[8,1,256]{2,1,0:T(1,128)}), f32[8,1,256]{2,1,0:T(1,128)S(1)}, u32[]{:S(2)}, u32[]{:S(2)}) %all-to-all-start.1) | async-done | bytes 8224 | tf_op jit(solution)/shard_map/all_to_all | solution.py:38
  95.1 0.5 broadcast.117
  95.6 0.7 reduce.18
  96.3 0.1 reshape.263
  96.4 0.1 reshape.226
  96.4 0.1 copy.62
  96.6 2.3 %scatter_custom_fusion.1 = f32[4,512]{0,1:T(8,128)S(1)} fusion(s32[512]{0:T(512)S(1)} %reshape.227, f32[512,4]{1,0:T(8,128)S(1)} %copy.62, f32[]{:T(128)} %constant.10.clone.1), kind=kCustom, calls=%fused_computation.21 | custom fusion | flops 2048 | bytes 8196 | tf_op jit(solution)/shard_map/vmap()/scatter-add | solution.py:42
  98.9 0.3 slice_reduce_fusion
  99.2 0.8 fusion
  100.0 1.0 gather_fusion.2
  101.1 0.1 copy.63
  101.2 0.7 reshape.264
  101.9 3.3 %all-to-all-start.2 = ((f32[8,1,192]{2,1,0:T(1,128)}), f32[8,1,192]{2,1,0:T(1,128)S(1)}, u32[]{:S(2)}, u32[]{:S(2)}) async-start(f32[8,1,192]{2,1,0:T(1,128)} %reshape.264), calls=%async_computation.2 | async-start | bytes 16384 | tf_op jit(solution)/shard_map/all_to_all | solution.py:47
  105.3 0.6 reshape_add_fusion
  105.9 0.1 reshape.192
  106.0 0.7 copy.68
  107.3 4.4 %all-to-all-done.2 = f32[8,1,192]{2,1,0:T(1,128)S(1)} async-done(((f32[8,1,192]{2,1,0:T(1,128)}), f32[8,1,192]{2,1,0:T(1,128)S(1)}, u32[]{:S(2)}, u32[]{:S(2)}) %all-to-all-start.2) | async-done | bytes 6176 | tf_op jit(solution)/shard_map/all_to_all | solution.py:47
  111.7 0.7 reduce.19
  112.4 0.1 reshape.265
  112.5 0.2 copy.67
  112.6 0.1 all_to_all.28
  112.7 0.7 fusion.4
  113.5 0.0 copy-done.6
  113.5 0.6 copy.69
  114.1 38.9 %all-reduce = (f32[1]{0:T(128)}, f32[1]{0:T(128)}) all-reduce(f32[1]{0:T(128)} %bitcast.22, f32[1]{0:T(128)} %bitcast.21), channel_id=1, replica_groups=mesh['robot'=8,'sub'=4] {'robot','sub'}, use_global_device_ids=true, to_apply=%region_7.0 | all-reduce | flops 2 | bytes 16 | tf_op jit(solution)/shard_map/psum | solution.py:53
  153.0 1.9 %fusion.10 = f32[2]{0:T(128)} fusion(f32[1]{0:T(128)} %get-tuple-element.22, f32[1]{0:T(128)} %get-tuple-element.23), kind=kLoop, calls=%fused_computation.41 | loop fusion | flops 4 | bytes 16 | tf_op jit(solution)/shard_map/sqrt | solution.py:55
  (27 shorter events, 0.2 us)
Async XLA Ops:
  3.2 79.4 %all-to-all-start = ((s32[1,8,64]{2,0,1:T(1,128)}), s32[1,8,64]{2,0,1:T(1,128)S(1)}, u32[]{:S(2)}, u32[]{:S(2)}) async-start(s32[1,8,64]{2,0,1:T(1,128)} %all_to_all.22), calls=%async_computation | async-start | bytes 8192 | tf_op jit(solution)/shard_map/all_to_all | solution.py:39
  33.0 2.3 %copy-start.1 = (f32[1,1,18,4096]{3,1,2,0:T(1,128)S(1)}, f32[1,1,18,4096]{3,1,2,0:T(1,128)}, u32[]{:S(2)}) copy-start(f32[1,1,18,4096]{3,1,2,0:T(1,128)} %param.20) | copy-start | bytes 884740
  35.2 2.8 %copy-start.3 = (f32[1,1,6,1024]{3,1,2,0:T(1,128)S(1)}, f32[1,1,6,1024]{3,1,2,0:T(1,128)}, u32[]{:S(2)}) copy-start(f32[1,1,6,1024]{3,1,2,0:T(1,128)} %param.18) | copy-start | bytes 73732
  38.1 16.0 %copy-start.9 = (s32[1,1,1024]{2,1,0:T(1,128)S(1)}, s32[1,1,1024]{2,1,0:T(1,128)}, u32[]{:S(2)}) copy-start(s32[1,1,1024]{2,1,0:T(1,128)} %param.24) | copy-start | bytes 12292
  38.1 16.0 %copy-start.5 = (f32[1,1,6,1024]{3,1,2,0:T(1,128)S(1)}, f32[1,1,6,1024]{3,1,2,0:T(1,128)}, u32[]{:S(2)}) copy-start(f32[1,1,6,1024]{3,1,2,0:T(1,128)} %param.25) | copy-start | bytes 73732
  38.1 19.9 %copy-start.7 = (s32[1,1,4096]{2,1,0:T(1,128)S(1)}, s32[1,1,4096]{2,1,0:T(1,128)}, u32[]{:S(2)}) copy-start(s32[1,1,4096]{2,1,0:T(1,128)} %param.22) | copy-start | bytes 49156
  57.9 23.0 %copy-start = (f32[1,1,6,1024]{2,3,1,0:T(8,128)S(1)}, f32[1,1,6,1024]{2,3,1,0:T(8,128)}, u32[]{:S(2)}) copy-start(f32[1,1,6,1024]{2,3,1,0:T(8,128)} %copy.57) | copy-start | bytes 73732
  58.0 23.2 %copy-start.2 = (f32[1,1,36,1024]{3,1,2,0:T(1,128)S(1)}, f32[1,1,36,1024]{3,1,2,0:T(1,128)}, u32[]{:S(2)}) copy-start(f32[1,1,36,1024]{3,1,2,0:T(1,128)} %param.19) | copy-start | bytes 442372
  80.9 1.5 copy-start.8
  81.6 31.9 %copy-start.4 = (f32[1,1,3,512]{3,1,2,0:T(1,128)S(1)}, f32[1,1,3,512]{3,1,2,0:T(1,128)}, u32[]{:S(2)}) copy-start(f32[1,1,3,512]{3,1,2,0:T(1,128)} %param.13) | copy-start | bytes 18436
  81.6 31.9 %copy-start.6 = (f32[1,1,3,512]{3,1,2,0:T(1,128)S(1)}, f32[1,1,3,512]{3,1,2,0:T(1,128)}, u32[]{:S(2)}) copy-start(f32[1,1,3,512]{3,1,2,0:T(1,128)} %param.14) | copy-start | bytes 18436
  82.6 12.5 %all-to-all-start.1 = ((f32[8,1,256]{2,1,0:T(1,128)}), f32[8,1,256]{2,1,0:T(1,128)S(1)}, u32[]{:S(2)}, u32[]{:S(2)}) async-start(f32[8,1,256]{2,1,0:T(1,128)} %reshape.262), calls=%async_computation.1 | async-start | bytes 16384 | tf_op jit(solution)/shard_map/all_to_all | solution.py:38
  101.9 9.8 %all-to-all-start.2 = ((f32[8,1,192]{2,1,0:T(1,128)}), f32[8,1,192]{2,1,0:T(1,128)S(1)}, u32[]{:S(2)}, u32[]{:S(2)}) async-start(f32[8,1,192]{2,1,0:T(1,128)} %reshape.264), calls=%async_computation.2 | async-start | bytes 16384 | tf_op jit(solution)/shard_map/all_to_all | solution.py:47
where the time goes:
time: 156 us; the launch traced here: 155 us
  blocking collectives  54.7 us (35%)
  other arithmetic  40.4 us (26%)
  local copies, waits for them, and re-layouts  31.6 us (20%)
  starting transfers between devices  16.6 us (11%)
  waiting for transfers between devices  10.1 us (6%)
  between operations  1.6 us (1%)
    psum x1, blocking collectives, body(): primal_all, dual_all = lax.psum((primal, dualsum), ('robot', 'sub'))  38.9 us
    scatter-add x1, other arithmetic, body(): jax.ops.segment_sum(entries, pose_ids, num_segments=pose_count)  22.9 us
    all_gather x1, blocking collectives, body(): robot_all = lax.all_gather(pose_block, 'sub', axis=1, tiled=True)  15.8 us
    gather x1, local copies, waits for them, and re-layouts, body(): copies_at = copies[:, obs_slot[0, 0]]  14.1 us
    all_to_all x1, starting transfers between devices, body(): lax.all_to_all(slot_ids, 'robot', split_axis=1, concat_axis=1, tiled=True)  7.28 us
    unnamed x32, local copies, waits for them, and re-layouts  7.06 us
    all_to_all x1, starting transfers between devices, body(): lax.all_to_all(outgoing, 'robot', split_axis=1, concat_axis=1, tiled=True)  6.01 us
    all_to_all x1, waiting for transfers between devices, body(): lax.all_to_all(outgoing, 'robot', split_axis=1, concat_axis=1, tiled=True)  5.69 us
  transfers between devices with their start and end apart: 3, of which 2 were waited for; matrix products, arithmetic and copies ran while one was open for 38% of the time, Pallas kernels for 0%

commit v1 on v0

v1 whole, which is shorter than its diff:
```python
import functools

import jax
import jax.numpy as jnp
from jax import lax
from jax.experimental import pallas as pl
from jax.experimental.pallas import tpu as pltpu
from jax.sharding import PartitionSpec as P

penalty = 2.0
LANES = 128
SUBLANES = 8
FIELDS = 8
SHIFT = LANES.bit_length() - 1


def split3(value):
    high = value.astype(jnp.bfloat16).astype(jnp.float32)
    rest = value - high
    middle = rest.astype(jnp.bfloat16).astype(jnp.float32)
    low = (rest - middle).astype(jnp.bfloat16).astype(jnp.float32)
    return high, middle, low


def lookup(tables, index, out_rows):
    low = index & (LANES - 1)
    high = index >> SHIFT
    results = []
    for rows in tables:
        total = None
        for k, row in enumerate(rows):
            table = jnp.broadcast_to(row, (out_rows, LANES))
            got = jnp.take_along_axis(table, low, axis=1, mode="promise_in_bounds")
            total = got if total is None else jnp.where(high == k, got, total)
        results.append(total)
    return results


def segment_rows(values, index, chunks, out_rows):
    sub = lax.broadcasted_iota(jnp.int32, (out_rows, LANES), 0)
    lane_ids = lax.broadcasted_iota(jnp.int32, (LANES, LANES), 0)
    group = min(4, chunks)
    total = None
    for start in range(0, chunks, group):
        left, right = [], []
        for t in range(start, start + group):
            ids = index(t)
            high = jnp.broadcast_to(ids >> SHIFT, (out_rows, LANES)) == sub
            low = jnp.broadcast_to(ids & (LANES - 1), (LANES, LANES)) == lane_ids
            left.append(
                jnp.concatenate(
                    [
                        jnp.where(high, jnp.broadcast_to(row, (out_rows, LANES)), 0.0)
                        for row in values(t)
                    ],
                    axis=0,
                ).astype(jnp.bfloat16)
            )
            right.append(jnp.where(low, 1.0, 0.0).astype(jnp.bfloat16))
        part = lax.dot_general(
            jnp.concatenate(left, axis=1),
            jnp.concatenate(right, axis=1),
            (((1,), (1,)), ((), ())),
            preferred_element_type=jnp.float32,
        )
        total = part if total is None else total + part
    return total


def column_of(counts_ref, first, step, rows):
    sub = lax.broadcasted_iota(jnp.int32, (rows, LANES), 0)
    result = jnp.zeros((rows, LANES), jnp.int32)
    for k in range(rows):
        result = jnp.where(sub == k, counts_ref[0, first + step * k], result)
    return result


def pack_kernel(block, counts_ref, copies_ref, duals_ref, ids_ref, out_ref):
    rows = ids_ref.shape[0]
    per = LANES // block
    lane = lax.broadcasted_iota(jnp.int32, (rows, LANES), 1)
    sources = [copies_ref[k] for k in range(3)] + [duals_ref[k] for k in range(3)]
    sources.append(ids_ref[...].astype(jnp.float32))
    for j in range(per):
        for v, source in enumerate(sources):
            moved = pltpu.roll(source, LANES - j * block, 1) if j else source
            out_ref[pl.ds(j * FIELDS + v, rows, per * FIELDS), :] = moved
        live = (lane < column_of(counts_ref, j, per, rows)).astype(jnp.float32)
        out_ref[pl.ds(j * FIELDS + 7, rows, per * FIELDS), :] = live


def owner_kernel(block, subs, recv_ref, old_ref, consensus_ref, out_ref):
    robots = recv_ref.shape[0] // FIELDS
    rows = old_ref.shape[1]
    padded = max(rows, SUBLANES)
    field = [recv_ref[pl.ds(v, robots, FIELDS), :] for v in range(FIELDS)]
    live = field[7]
    ids = field[6].astype(jnp.int32)
    pieces = [split3(live * (field[v] + field[3 + v])) for v in range(3)]
    planes = [pieces[v][s] for s in range(3) for v in range(3)] + [live]
    sums = segment_rows(
        lambda t: [plane[t : t + 1] for plane in planes],
        lambda t: ids[t : t + 1],
        robots,
        padded,
    )

    def plane_sum(j):
        return sums[j * padded : j * padded + rows]

    seen = plane_sum(9)
    weight = 1.0 + seen
    dual_sum = jnp.zeros((rows, LANES), jnp.float32)
    tables = []
    for v in range(3):
        old = old_ref[v]
        new = (old + (plane_sum(v) + (plane_sum(3 + v) + plane_sum(6 + v)))) / weight
        consensus_ref[v] = new
        change = new - old
        dual_sum = dual_sum + seen * change * change
        tables.append([new[k : k + 1] for k in range(rows)])
    back = lookup(tables, ids, robots)
    primal = jnp.zeros((robots, LANES), jnp.float32)
    for v in range(3):
        differ = (field[v] - back[v]) * live
        primal = primal + differ * differ
    primal = jnp.sum(primal, axis=(0, 1), keepdims=True)
    dual_sum = penalty * penalty * jnp.sum(dual_sum, axis=(0, 1), keepdims=True)
    lane = lax.broadcasted_iota(jnp.int32, (robots, LANES), 1)
    first = jnp.where(lane < block, back[0], pltpu.roll(back[1], block, 1))
    sums_row = jnp.where(lane == block, primal, jnp.where(lane == block + 1, dual_sum, 0.0))
    second = jnp.where(lane < block, back[2], sums_row)
    for s in range(subs):
        out_ref[pl.ds(2 * s, robots, 2 * subs), :] = first
        out_ref[pl.ds(2 * s + 1, robots, 2 * subs), :] = second


def observe_kernel(copies_ref, measured_ref, jac_ref, slot_ref, pose_ref, out_ref, planes_ref):
    rows = slot_ref.shape[0]
    table_rows = copies_ref.shape[1]
    out_rows = out_ref.shape[1]
    for start in range(0, rows, SUBLANES):
        part = pl.ds(start, SUBLANES)
        tables = [[copies_ref[k, pl.ds(j, 1), :] for j in range(table_rows)] for k in range(3)]
        at = lookup(tables, slot_ref[part, :], SUBLANES)
        error = [measured_ref[k, part, :] - at[k] for k in range(3)]
        for a in range(6):
            pull = (
                jac_ref[a, part, :] * error[0]
                + jac_ref[6 + a, part, :] * error[1]
                + jac_ref[12 + a, part, :] * error[2]
            )
            for s, piece in enumerate(split3(pull)):
                planes_ref[s * 6 + a, part, :] = piece
    sums = segment_rows(
        lambda t: [planes_ref[j, pl.ds(t, 1), :] for j in range(18)],
        lambda t: pose_ref[pl.ds(t, 1), :],
        rows,
        out_rows,
    )
    for a in range(6):
        high, middle, low = (
            sums[(s * 6 + a) * out_rows : (s * 6 + a + 1) * out_rows] for s in range(3)
        )
        out_ref[a] = high + (middle + low)


def refine_kernel(all_ref, pose_ref, grad_ref, inverse_ref, edge_ref, offset_ref, out_ref):
    subs = all_ref.shape[0]
    rows = edge_ref.shape[0]
    tables = [
        [all_ref[s, a, pl.ds(k, 1), :] for s in range(subs) for k in range(rows)] for a in range(6)
    ]
    far = lookup(tables, edge_ref[...], rows)
    grad = [grad_ref[a] + far[a] - pose_ref[a] - offset_ref[a] for a in range(6)]
    for a in range(6):
        delta = inverse_ref[a * 6] * grad[0]
        for b in range(1, 6):
            delta = delta + inverse_ref[a * 6 + b] * grad[b]
        out_ref[a] = pose_ref[a] + delta


def finish_kernel(
    block, subs, landmark_total, where_ref, counts_ref, recv_ref, copies_ref, duals_ref,
    dual_ref, norm_ref,
):
    rows = copies_ref.shape[1]
    per = LANES // block
    robots = rows * per
    me = where_ref[0]
    lane = lax.broadcasted_iota(jnp.int32, (rows, LANES), 1)
    back = [jnp.zeros((rows, LANES), jnp.float32) for _ in range(3)]
    live = jnp.zeros((rows, LANES), jnp.bool_)
    for j in range(per):
        here = (lane >= j * block) & (lane < (j + 1) * block)
        live = live | (here & (lane - j * block < column_of(counts_ref, j, per, rows)))
        for v, (line, at) in enumerate(((0, 0), (0, block), (1, 0))):
            start = 2 * (j * subs + me) + line
            got = recv_ref[pl.ds(start, rows, 2 * subs * per), :]
            turn = (j * block - at) % LANES
            moved = pltpu.roll(got, turn, 1) if turn else got
            back[v] = jnp.where(here, moved, back[v])
    for v in range(3):
        differ = jnp.where(live, copies_ref[v] - back[v], 0.0)
        dual_ref[v] = duals_ref[v] + differ
    sums = jnp.sum(recv_ref[pl.ds(1, robots * subs, 2), :], axis=0, keepdims=True)
    norms = jnp.sqrt(sums / landmark_total)
    lane = lax.broadcasted_iota(jnp.int32, (1, LANES), 1)
    for k in range(2):
        norm_ref[k] = jnp.sum(jnp.where(lane == block + k, norms, 0.0))


VMEM = pl.BlockSpec(memory_space=pltpu.VMEM)
SMEM = pl.BlockSpec(memory_space=pltpu.SMEM)


def call(kernel, outs, in_specs, name, out_specs=None, scratch=()):
    shapes = [jax.ShapeDtypeStruct(shape, jnp.float32) for shape in outs]
    return pl.pallas_call(
        kernel,
        out_shape=shapes,
        in_specs=in_specs,
        out_specs=out_specs or [VMEM] * len(outs),
        scratch_shapes=list(scratch),
        name=name,
    )


def body(
    landmark_copies,
    dual_copies,
    visibility,
    block_counts,
    consensus_old,
    poses,
    inverse_blocks,
    jacobians,
    measurements,
    obs_pose,
    obs_slot,
    edge_to,
    edge_offset,
):
    robots = lax.axis_size("robot")
    subs = lax.axis_size("sub")
    slots = landmark_copies.shape[3]
    owned = consensus_old.shape[3]
    pose_count = poses.shape[3]
    observed = obs_slot.shape[2]
    block = slots // robots
    rows, owned_rows = slots // LANES, owned // LANES
    pose_rows, obs_rows = pose_count // LANES, observed // LANES

    copies = landmark_copies.reshape(3, rows, LANES)
    duals = dual_copies.reshape(3, rows, LANES)
    ids = visibility.reshape(rows, LANES)
    counts = block_counts.reshape(1, robots)
    old = consensus_old.reshape(3, owned_rows, LANES)
    pose_block = poses.reshape(6, pose_rows, LANES)
    inverse = inverse_blocks.reshape(36, pose_rows, LANES)
    jac = jacobians.reshape(18, obs_rows, LANES)
    measured = measurements.reshape(3, obs_rows, LANES)
    pose_ids = obs_pose.reshape(obs_rows, LANES)
    slot_ids = obs_slot.reshape(obs_rows, LANES)
    edges = edge_to.reshape(pose_rows, LANES)
    offset = edge_offset.reshape(6, pose_rows, LANES)

    (outgoing,) = call(
        functools.partial(pack_kernel, block),
        [(robots * FIELDS, LANES)],
        [SMEM, VMEM, VMEM, VMEM],
        "pack",
    )(counts, copies, duals, ids)
    received = lax.all_to_all(
        outgoing.reshape(robots, FIELDS, LANES), "robot", 0, 0, tiled=True
    ).reshape(robots * FIELDS, LANES)

    everyone = lax.all_to_all(
        jnp.broadcast_to(pose_block[None], (subs, 6, pose_rows, LANES)), "sub", 0, 0, tiled=True
    )
    (grad_obs,) = call(
        observe_kernel,
        [(6, pose_rows, LANES)],
        [VMEM] * 5,
        "observe",
        scratch=[pltpu.VMEM((18, obs_rows, LANES), jnp.float32)],
    )(copies, measured, jac, slot_ids, pose_ids)

    consensus, returning = call(
        functools.partial(owner_kernel, block, subs),
        [(3, owned_rows, LANES), (robots * subs * 2, LANES)],
        [VMEM, VMEM],
        "owner",
    )(received, old)
    back = lax.all_to_all(
        returning.reshape(robots * subs, 2, LANES), ("robot", "sub"), 0, 0, tiled=True
    ).reshape(robots * subs * 2, LANES)

    (refined,) = call(
        refine_kernel, [(6, pose_rows, LANES)], [VMEM] * 6, "refine"
    )(everyone, pose_block, grad_obs, inverse, edges, offset)

    where = lax.axis_index("sub").astype(jnp.int32).reshape(1)
    dual_new, residual_norms = call(
        functools.partial(finish_kernel, block, subs, float(owned * robots * subs)),
        [(3, rows, LANES), (2,)],
        [SMEM, SMEM, VMEM, VMEM, VMEM],
        "finish",
        out_specs=[VMEM, SMEM],
    )(where, counts, back, copies, duals)
    return (
        refined.reshape(1, 1, 6, pose_count),
        consensus.reshape(1, 1, 3, owned),
        dual_new.reshape(1, 1, 3, slots),
        residual_norms,
    )


def solution(mesh):
    split4 = P("robot", "sub", None, None)
    split3d = P("robot", "sub", None)
    return jax.shard_map(
        body,
        mesh=mesh,
        in_specs=(
            split4,
            split4,
            split3d,
            split3d,
            split4,
            split4,
            split4,
            split4,
            split4,
            split3d,
            split3d,
            split3d,
            split4,
        ),
        out_specs=(split4, split4, split4, P()),
        check_vma=False,
    )
```

time: 156 us -> 37 us (0.24)
  blocking collectives: 54.7 us -> 14.2 us
  other arithmetic: 40.4 us -> 0 us
  local copies, waits for them, and re-layouts: 31.6 us -> 1.25 us
  starting transfers between devices: 16.6 us -> 5.83 us
  Pallas kernels: 0 us -> 8.92 us
  waiting for transfers between devices: 10.1 us -> 5.58 us
    psum x1 -> x0, blocking collectives: 38.9 us -> none  [body(): primal_all, dual_all = lax.psum((primal, dualsum), ('robot', 'sub'))]
    scatter-add x2 -> x0, other arithmetic: 25.2 us -> none  [the longest x1 22.9 us: body(): jax.ops.segment_sum(entries, pose_ids, num_segments=pose_count)]
    gather x3 -> x0, local copies, waits for them, and re-layouts: 17.9 us -> none  [the longest x1 14.1 us: body(): copies_at = copies[:, obs_slot[0, 0]]]
    all_gather x1 -> x0, blocking collectives: 15.8 us -> none  [body(): robot_all = lax.all_gather(pose_block, 'sub', axis=1, tiled=True)]
    all_to_all x0 -> x1, blocking collectives: none -> 14.2 us  [body(): lax.all_to_all(outgoing.reshape(robots, FIELDS, LANES), 'robot', 0, 0, ti...]
    all_to_all x3 -> x2, starting transfers between devices: 16.6 us -> 5.83 us  [the longest x1 3.3 us: body(): lax.all_to_all(jnp.broadcast_to(pose_block[None], (subs, 6, pose_rows, LA...]
    pallas_call x0 -> x5, Pallas kernels: none -> 8.92 us  [the longest x1 2.22 us: body(): call(observe_kernel, [(6, pose_rows, LANES)], [VMEM] * 5, 'observe', scra...]
    unnamed x32 -> x6, local copies, waits for them, and re-layouts: 7.06 us -> 0.61 us
  transfers between devices with their start and end apart: 3 -> 2, of which waited for: 2 -> 2; matrix products, arithmetic and copies ran while one was open for 38% -> 0% of each run, Pallas kernels for 0% -> 16%
where the time goes in v1:
time: 37 us; the launch traced here: 36.4 us
  blocking collectives  14.2 us (38%)
  Pallas kernels  8.92 us (24%)
  starting transfers between devices  5.83 us (16%)
  waiting for transfers between devices  5.58 us (15%)
  local copies, waits for them, and re-layouts  1.25 us (3%)
  between operations  0.66 us (2%)
    all_to_all x1, blocking collectives, body(): lax.all_to_all(outgoing.reshape(robots, FIELDS, LANES), 'robot', 0, 0, ti...  14.2 us
    all_to_all x1, starting transfers between devices, body(): lax.all_to_all(jnp.broadcast_to(pose_block[None], (subs, 6, pose_rows, LA...  3.3 us
    all_to_all x1, waiting for transfers between devices, body(): lax.all_to_all(returning.reshape(robots * subs, 2, LANES), ('robot', 'sub...  3.15 us
    all_to_all x1, starting transfers between devices, body(): lax.all_to_all(returning.reshape(robots * subs, 2, LANES), ('robot', 'sub...  2.52 us
    all_to_all x1, waiting for transfers between devices, body(): lax.all_to_all(jnp.broadcast_to(pose_block[None], (subs, 6, pose_rows, LA...  2.43 us
    pallas_call x1, Pallas kernels, body(): call(observe_kernel, [(6, pose_rows, LANES)], [VMEM] * 5, 'observe', scra...  2.22 us
    pallas_call x1, Pallas kernels, body(): call(refine_kernel, [(6, pose_rows, LANES)], [VMEM] * 6, 'refine')  1.88 us
    pallas_call x1, Pallas kernels, body(): call(functools.partial(owner_kernel, block, subs), [(3, owned_rows, LANES...  1.83 us
  transfers between devices with their start and end apart: 2, of which 2 were waited for; matrix products, arithmetic and copies ran while one was open for 0% of the time, Pallas kernels for 16%

profile of v1, /device:TPU:0, one launch (start us, length us, event | category | flops | bytes accessed | tf_op | source)
XLA Modules:
  0.0 36.4 jit_solution(9487278979164884917)
XLA Ops:
  0.6 1.5 %pack.1 = f32[64,128]{1,0:T(8,128)} custom-call(s32[1,8]{1,0:T(1,128)} %bitcast.41, f32[3,4,128]{2,1,0:T(4,128)} %bitcast.28, f32[3,4,128]{2,1,0:T(4,128)} %bitcast.33, s32[4,128]{1,0:T(4,128)} %bitcast.43), custom_call_target="tpu_custom_call" | custom-call | tf_op jit(solution)/shard_map/pack/pallas_call | solution.py:268
  2.1 0.0 copy-start.2
  2.1 14.2 %all_to_all.15 = f32[8,8,128]{2,1,0:T(8,128)} all-to-all(f32[8,8,128]{2,1,0:T(8,128)} %bitcast.25), channel_id=1, replica_groups=mesh['robot'=8,'sub'=4] {'robot'}, dimensions={0} | all-to-all | bytes 65536 | tf_op jit(solution)/shard_map/all_to_all | solution.py:274
  16.3 0.0 copy-done.2
  16.3 0.6 %broadcast_in_dim.8 = f32[4,6,8,128]{3,2,1,0:T(8,128)} broadcast(f32[6,8,128]{2,1,0:T(8,128)S(1)} %bitcast.27), dimensions={1,2,3} | broadcast | bytes 122880 | tf_op jit(solution)/shard_map/broadcast_in_dim | solution.py:279
  17.0 3.3 %all-to-all-start = ((f32[4,6,8,128]{3,2,1,0:T(8,128)}), f32[4,6,8,128]{3,2,1,0:T(8,128)S(1)}, u32[]{:S(2)}, u32[]{:S(2)}) async-start(f32[4,6,8,128]{3,2,1,0:T(8,128)} %broadcast_in_dim.8), calls=%async_computation | async-start | bytes 196608 | tf_op jit(solution)/shard_map/all_to_all | solution.py:278
  20.3 1.8 %owner.1 = (f32[3,4,128]{2,1,0:T(4,128)}, f32[64,128]{1,0:T(8,128)}) custom-call(f32[64,128]{1,0:T(8,128)} %bitcast.24, f32[3,4,128]{2,1,0:T(4,128)} %bitcast.39), custom_call_target="tpu_custom_call" | custom-call | tf_op jit(solution)/shard_map/owner/pallas_call | solution.py:289
  22.1 2.4 %all-to-all-done.all_ref = f32[4,6,8,128]{3,2,1,0:T(8,128)S(1)} async-done(((f32[4,6,8,128]{3,2,1,0:T(8,128)}), f32[4,6,8,128]{3,2,1,0:T(8,128)S(1)}, u32[]{:S(2)}, u32[]{:S(2)}) %all-to-all-start) | async-done | bytes 98336 | tf_op jit(solution)/shard_map/all_to_all | solution.py:278
  24.5 0.0 copy-start
  24.5 2.5 %all-to-all-start.2 = ((f32[32,2,128]{2,1,0:T(2,128)}), f32[32,2,128]{2,1,0:T(2,128)S(1)}, u32[]{:S(2)}, u32[]{:S(2)}) async-start(f32[32,2,128]{2,1,0:T(2,128)} %bitcast.32), calls=%async_computation.2 | async-start | bytes 65536 | tf_op jit(solution)/shard_map/all_to_all | solution.py:295
  27.1 2.2 %observe.1.grad_ref = f32[6,8,128]{2,1,0:T(8,128)} custom-call(f32[3,4,128]{2,1,0:T(4,128)} %bitcast.29, f32[3,32,128]{2,1,0:T(8,128)} %bitcast.31, f32[18,32,128]{2,1,0:T(8,128)} %bitcast.21, s32[32,128]{1,0:T(8,128)} %bitcast.37, s32[32,128]{1,0:T(8,128)} %bitcast.38), custom_call_target="tpu_custom_call" | custom-call | tf_op jit(solution)/shard_map/observe/pallas_call | solution.py:281
  29.3 0.0 copy-done
  29.3 1.9 %refine.1 = f32[6,8,128]{2,1,0:T(8,128)} custom-call(f32[4,6,8,128]{3,2,1,0:T(8,128)} %copy-done, f32[6,8,128]{2,1,0:T(8,128)} %bitcast.26, f32[6,8,128]{2,1,0:T(8,128)} %observe.1.grad_ref, f32[36,8,128]{2,1,0:T(8,128)} %bitcast.22, s32[8,128]{1,0:T(8,128)} %bitcast.40, f32[6,8,128]{2,1,0:T(8,128)} %bitcast.35), custom_call_target="tpu_custom_call" | custom-call | tf_op jit(solution)/shard_map/refine/pallas_call | solution.py:299
  31.2 3.1 %all-to-all-done.2 = f32[32,2,128]{2,1,0:T(2,128)S(1)} async-done(((f32[32,2,128]{2,1,0:T(2,128)}), f32[32,2,128]{2,1,0:T(2,128)S(1)}, u32[]{:S(2)}, u32[]{:S(2)}) %all-to-all-start.2) | async-done | bytes 32800 | tf_op jit(solution)/shard_map/all_to_all | solution.py:295
  34.3 0.0 copy-start.1
  34.3 0.6 %copy-done.1 = f32[32,2,128]{2,1,0:T(2,128)} copy-done((f32[32,2,128]{2,1,0:T(2,128)}, f32[32,2,128]{2,1,0:T(2,128)S(1)}, u32[]{:S(2)}) %copy-start.1) | copy-done | bytes 32792
  34.9 1.5 %finish.1 = (f32[3,4,128]{2,1,0:T(4,128)}, f32[2]{0:T(128)}) custom-call(s32[1]{0:T(128)} %bitcast.17.where_ref, s32[1,8]{1,0:T(1,128)} %bitcast.42, f32[64,128]{1,0:T(8,128)} %bitcast.23, f32[3,4,128]{2,1,0:T(4,128)} %bitcast.30, f32[3,4,128]{2,1,0:T(4,128)} %bitcast.34), custom_call_target="tpu_custom_call" | custom-call | tf_op jit(solution)/shard_map/finish/pallas_call | solution.py:304
Async XLA Ops:
  2.1 14.2 %copy-start.2 = (f32[1,1,6,1024]{3,1,2,0:T(1,128)S(1)}, f32[1,1,6,1024]{3,1,2,0:T(1,128)}, u32[]{:S(2)}) copy-start(f32[1,1,6,1024]{3,1,2,0:T(1,128)} %param.18) | copy-start | bytes 73732
  17.0 7.6 %all-to-all-start = ((f32[4,6,8,128]{3,2,1,0:T(8,128)}), f32[4,6,8,128]{3,2,1,0:T(8,128)S(1)}, u32[]{:S(2)}, u32[]{:S(2)}) async-start(f32[4,6,8,128]{3,2,1,0:T(8,128)} %broadcast_in_dim.8), calls=%async_computation | async-start | bytes 196608 | tf_op jit(solution)/shard_map/all_to_all | solution.py:278
  24.5 4.8 %copy-start = (f32[4,6,8,128]{3,2,1,0:T(8,128)}, f32[4,6,8,128]{3,2,1,0:T(8,128)S(1)}, u32[]{:S(2)}) copy-start(f32[4,6,8,128]{3,2,1,0:T(8,128)S(1)} %all-to-all-done.all_ref) | copy-start | bytes 294916
  24.5 9.8 %all-to-all-start.2 = ((f32[32,2,128]{2,1,0:T(2,128)}), f32[32,2,128]{2,1,0:T(2,128)S(1)}, u32[]{:S(2)}, u32[]{:S(2)}) async-start(f32[32,2,128]{2,1,0:T(2,128)} %bitcast.32), calls=%async_computation.2 | async-start | bytes 65536 | tf_op jit(solution)/shard_map/all_to_all | solution.py:295
  34.3 0.6 %copy-start.1 = (f32[32,2,128]{2,1,0:T(2,128)}, f32[32,2,128]{2,1,0:T(2,128)S(1)}, u32[]{:S(2)}) copy-start(f32[32,2,128]{2,1,0:T(2,128)S(1)} %all-to-all-done.2) | copy-start | bytes 98308

commit v2 on v1

--- a/solution.py
+++ b/solution.py
@@ -6,6 +6,7 @@
 from jax.experimental import pallas as pl
 from jax.experimental.pallas import tpu as pltpu
 from jax.sharding import PartitionSpec as P
+
 
 penalty = 2.0
 LANES = 128
@@ -165,13 +166,18 @@
         out_ref[a] = high + (middle + low)
 
 
-def refine_kernel(all_ref, pose_ref, grad_ref, inverse_ref, edge_ref, offset_ref, out_ref):
-    subs = all_ref.shape[0]
+def refine_kernel(where_ref, edge_ref, grad_ref, inverse_ref, offset_ref, *refs):
+    blocks, out_ref = refs[:-1], refs[-1]
+    pose_ref = blocks[0]
+    subs = len(blocks)
     rows = edge_ref.shape[0]
+    count = rows * LANES
+    edge = edge_ref[...]
+    place = lax.rem(where_ref[0] + subs - edge // count, subs)
     tables = [
-        [all_ref[s, a, pl.ds(k, 1), :] for s in range(subs) for k in range(rows)] for a in range(6)
+        [held[a, pl.ds(k, 1), :] for held in blocks for k in range(rows)] for a in range(6)
     ]
-    far = lookup(tables, edge_ref[...], rows)
+    far = lookup(tables, place * count + lax.rem(edge, count), rows)
     grad = [grad_ref[a] + far[a] - pose_ref[a] - offset_ref[a] for a in range(6)]
     for a in range(6):
         delta = inverse_ref[a * 6] * grad[0]
@@ -214,19 +220,25 @@
 SMEM = pl.BlockSpec(memory_space=pltpu.SMEM)
 
 
-def call(kernel, outs, in_specs, name, out_specs=None, scratch=()):
-    shapes = [jax.ShapeDtypeStruct(shape, jnp.float32) for shape in outs]
+def in_vmem(value):
+    return pltpu.with_memory_space_constraint(value, pltpu.VMEM)
+
+
+def call(kernel, outs, in_specs, out_specs=None, scratch=()):
+    shapes = [
+        jax.ShapeDtypeStruct(shape, jnp.float32) if isinstance(shape, tuple) else shape
+        for shape in outs
+    ]
     return pl.pallas_call(
         kernel,
         out_shape=shapes,
         in_specs=in_specs,
         out_specs=out_specs or [VMEM] * len(outs),
         scratch_shapes=list(scratch),
-        name=name,
-    )
-
-
-def body(
+    )
+
+
+def step(
     landmark_copies,
     dual_copies,
     visibility,
@@ -265,49 +277,50 @@
     edges = edge_to.reshape(pose_rows, LANES)
     offset = edge_offset.reshape(6, pose_rows, LANES)
 
+    where = lax.axis_index("sub").astype(jnp.int32).reshape(1)
+    held = [pose_block]
+    for k in range(1, subs):
+        ring = [(i, (i + k) % subs) for i in range(subs)]
+        held.append(lax.ppermute(pose_block, "sub", ring))
+
     (outgoing,) = call(
         functools.partial(pack_kernel, block),
-        [(robots * FIELDS, LANES)],
+        [pltpu.VMEM((robots * FIELDS, LANES), jnp.float32)],
         [SMEM, VMEM, VMEM, VMEM],
-        "pack",
     )(counts, copies, duals, ids)
     received = lax.all_to_all(
         outgoing.reshape(robots, FIELDS, LANES), "robot", 0, 0, tiled=True
     ).reshape(robots * FIELDS, LANES)
 
-    everyone = lax.all_to_all(
-        jnp.broadcast_to(pose_block[None], (subs, 6, pose_rows, LANES)), "sub", 0, 0, tiled=True
-    )
     (grad_obs,) = call(
         observe_kernel,
-        [(6, pose_rows, LANES)],
+        [pltpu.VMEM((6, pose_rows, LANES), jnp.float32)],
         [VMEM] * 5,
-        "observe",
         scratch=[pltpu.VMEM((18, obs_rows, LANES), jnp.float32)],
     )(copies, measured, jac, slot_ids, pose_ids)
 
     consensus, returning = call(
         functools.partial(owner_kernel, block, subs),
-        [(3, owned_rows, LANES), (robots * subs * 2, LANES)],
+        [
+            pltpu.VMEM((3, owned_rows, LANES), jnp.float32),
+            pltpu.VMEM((robots * subs * 2, LANES), jnp.float32),
+        ],
         [VMEM, VMEM],
-        "owner",
-    )(received, old)
+    )(in_vmem(received), in_vmem(old))
     back = lax.all_to_all(
         returning.reshape(robots * subs, 2, LANES), ("robot", "sub"), 0, 0, tiled=True
     ).reshape(robots * subs * 2, LANES)
 
     (refined,) = call(
-        refine_kernel, [(6, pose_rows, LANES)], [VMEM] * 6, "refine"
-    )(everyone, pose_block, grad_obs, inverse, edges, offset)
-
-    where = lax.axis_index("sub").astype(jnp.int32).reshape(1)
+        refine_kernel, [(6, pose_rows, LANES)], [SMEM] + [VMEM] * (4 + subs)
+    )(where, edges, in_vmem(grad_obs), inverse, offset, *held)
+
     dual_new, residual_norms = call(
         functools.partial(finish_kernel, block, subs, float(owned * robots * subs)),
         [(3, rows, LANES), (2,)],
         [SMEM, SMEM, VMEM, VMEM, VMEM],
-        "finish",
         out_specs=[VMEM, SMEM],
-    )(where, counts, back, copies, duals)
+    )(where, counts, in_vmem(back), in_vmem(copies), in_vmem(duals))
     return (
         refined.reshape(1, 1, 6, pose_count),
         consensus.reshape(1, 1, 3, owned),
@@ -320,7 +333,7 @@
     split4 = P("robot", "sub", None, None)
     split3d = P("robot", "sub", None)
     return jax.shard_map(
-        body,
+        step,
         mesh=mesh,
         in_specs=(
             split4,

time: 37 us -> 29.1 us (0.79)
  waiting for transfers between devices: 5.58 us -> 0.01 us
  Pallas kernels: 8.92 us -> 6.74 us
    all_to_all x2 -> x1, waiting for transfers between devices: 5.58 us -> 0.01 us  [step(): lax.all_to_all(returning.reshape(robots * subs, 2, LANES), ('robot', 'sub...]
    all_to_all x2 -> x1, starting transfers between devices: 5.83 us -> 2.65 us  [step(): lax.all_to_all(returning.reshape(robots * subs, 2, LANES), ('robot', 'sub...]
    ppermute x0 -> x3, starting transfers between devices: none -> 3.17 us  [step(): held.append(lax.ppermute(pose_block, 'sub', ring))]
    pallas_call x5, Pallas kernels: 8.92 us -> 6.74 us  [the longest x1 1.82 us: step(): call(refine_kernel, [(6, pose_rows, LANES)], [SMEM] + [VMEM] * (4 + subs))]
    unnamed x6 -> x15, local copies, waits for them, and re-layouts: 0.61 us -> 1.32 us
    broadcast_in_dim x1 -> x0, local copies, waits for them, and re-layouts: 0.64 us -> none  [body(): jnp.broadcast_to(pose_block[None], (subs, 6, pose_rows, LANES))]
  transfers between devices with their start and end apart: 2 -> 4, of which waited for: 2 -> 0; matrix products, arithmetic and copies ran while one was open for 0% -> 2% of each run, Pallas kernels for 16% -> 12%
where the time goes in v2:
time: 29.1 us; the launch traced here: 28.5 us
  blocking collectives  13.9 us (48%)
  Pallas kernels  6.74 us (23%)
  starting transfers between devices  5.82 us (20%)
  local copies, waits for them, and re-layouts  1.32 us (5%)
  between operations  0.71 us (2%)
    all_to_all x1, blocking collectives, step(): lax.all_to_all(outgoing.reshape(robots, FIELDS, LANES), 'robot', 0, 0, ti...  13.9 us
    ppermute x3, starting transfers between devices, step(): held.append(lax.ppermute(pose_block, 'sub', ring))  3.17 us
    all_to_all x1, starting transfers between devices, step(): lax.all_to_all(returning.reshape(robots * subs, 2, LANES), ('robot', 'sub...  2.65 us
    pallas_call x1, Pallas kernels, step(): call(refine_kernel, [(6, pose_rows, LANES)], [SMEM] + [VMEM] * (4 + subs))  1.82 us
    pallas_call x1, Pallas kernels, step(): call(observe_kernel, [pltpu.VMEM((6, pose_rows, LANES), jnp.float32)], [V...  1.61 us
    pallas_call x1, Pallas kernels, step(): call(functools.partial(finish_kernel, block, subs, float(owned * robots *...  1.37 us
    unnamed x15, local copies, waits for them, and re-layouts  1.32 us
    pallas_call x1, Pallas kernels, step(): call(functools.partial(owner_kernel, block, subs), [pltpu.VMEM((3, owned_...  1.06 us
  transfers between devices with their start and end apart: 4, of which 0 were waited for; matrix products, arithmetic and copies ran while one was open for 2% of the time, Pallas kernels for 12%

profile of v2, /device:TPU:0, one launch (start us, length us, event | category | flops | bytes accessed | tf_op | source)
XLA Modules:
  0.0 28.5 jit_solution(17850836209912020376)
XLA Ops:
  0.6 0.9 %shard_map.158 = f32[64,128]{1,0:T(8,128)S(1)} custom-call(s32[1,8]{1,0:T(1,128)} %bitcast.43, f32[3,4,128]{2,1,0:T(4,128)} %bitcast.25, f32[3,4,128]{2,1,0:T(4,128)} %bitcast.28, s32[4,128]{1,0:T(4,128)} %bitcast.45), custom_call_target="tpu_custom_call" | custom-call | tf_op jit(solution)/shard_map/pallas_call | solution.py:286
  1.5 0.0 copy-start.2
  1.5 13.9 %all_to_all.10 = f32[8,8,128]{2,1,0:T(8,128)S(1)} all-to-all(f32[8,8,128]{2,1,0:T(8,128)S(1)} %bitcast.24), channel_id=1, replica_groups=mesh['robot'=8,'sub'=4] {'robot'}, dimensions={0} | all-to-all | bytes 65536 | tf_op jit(solution)/shard_map/all_to_all | solution.py:291
  15.4 0.0 copy-done.2
  15.4 1.1 %shard_map.159 = (f32[3,4,128]{2,1,0:T(4,128)S(1)}, f32[64,128]{1,0:T(8,128)}) custom-call(f32[64,128]{1,0:T(8,128)S(1)} %bitcast.23, f32[3,4,128]{2,1,0:T(4,128)S(1)} %bitcast.30), custom_call_target="tpu_custom_call" | custom-call | tf_op jit(solution)/shard_map/pallas_call | solution.py:302
  16.5 0.0 copy-start.3
  16.5 2.6 %all-to-all-start.1 = ((f32[32,2,128]{2,1,0:T(2,128)}), f32[32,2,128]{2,1,0:T(2,128)S(1)}, u32[]{:S(2)}, u32[]{:S(2)}) async-start(f32[32,2,128]{2,1,0:T(2,128)} %bitcast.18), calls=%async_computation.1 | async-start | bytes 65536 | tf_op jit(solution)/shard_map/all_to_all | solution.py:310
  19.1 0.0 copy-done.3
  19.1 0.2 collective-permute-start
  19.3 1.7 %collective-permute-start.1 = (f32[6,8,128]{2,1,0:T(8,128)S(1)}, f32[6,8,128]{2,1,0:T(8,128)S(1)}, u32[]{:S(2)}, u32[]{:S(2)}) collective-permute-start(f32[6,8,128]{2,1,0:T(8,128)S(1)} %bitcast.37), channel_id=1, source_target_pairs={{0,2},{1,3},{2,0},{3,1},{4,6},{5,7},{6,4},{7,5},{8,10},{9,11},{10,... | collective-permute-start | bytes 73736 | tf_op jit(solution)/shard_map/ppermute | solution.py:284
  21.0 1.3 %collective-permute-start.2 = (f32[6,8,128]{2,1,0:T(8,128)S(1)}, f32[6,8,128]{2,1,0:T(8,128)S(1)}, u32[]{:S(2)}, u32[]{:S(2)}) collective-permute-start(f32[6,8,128]{2,1,0:T(8,128)S(1)} %bitcast.38), channel_id=1, source_target_pairs={{0,3},{1,0},{2,1},{3,2},{4,7},{5,4},{6,5},{7,6},{8,11},{9,8},{10,9... | collective-permute-start | bytes 73736 | tf_op jit(solution)/shard_map/ppermute | solution.py:284
  22.3 1.6 %shard_map.156.grad_ref = f32[6,8,128]{2,1,0:T(8,128)S(1)} custom-call(f32[3,4,128]{2,1,0:T(4,128)} %bitcast.26, f32[3,32,128]{2,1,0:T(8,128)} %bitcast.33, f32[18,32,128]{2,1,0:T(8,128)} %bitcast.31, s32[32,128]{1,0:T(8,128)} %bitcast.40, s32[32,128]{1,0:T(8,128)} %bitcast.41), custom_call_target="tpu_custom_call" | custom-call | tf_op jit(solution)/shard_map/pallas_call | solution.py:295
  23.9 0.0 collective-permute-done.refs_1_
  23.9 0.0 copy-start.4
  23.9 0.0 collective-permute-done.1.refs_2_
  24.0 0.0 copy-start.5
  24.0 0.0 collective-permute-done.2.refs_3_
  24.0 0.0 copy-start.6
  24.0 0.5 %copy-done.4 = f32[6,8,128]{2,1,0:T(8,128)} copy-done((f32[6,8,128]{2,1,0:T(8,128)}, f32[6,8,128]{2,1,0:T(8,128)S(1)}, u32[]{:S(2)}) %copy-start.4) | copy-done | bytes 24600
  24.5 0.0 copy-done.5
  24.6 0.0 copy-done.6
  24.6 1.8 %shard_map.157 = f32[6,8,128]{2,1,0:T(8,128)} custom-call(s32[1]{0:T(128)} %bitcast.where_ref, s32[8,128]{1,0:T(8,128)} %bitcast.42, f32[6,8,128]{2,1,0:T(8,128)S(1)} %shard_map.156.grad_ref, f32[36,8,128]{2,1,0:T(8,128)} %bitcast.32, f32[6,8,128]{2,1,0:T(8,128)} %bitcast.34, f32[6,8,128]{2,1,0:T(8,128)} %bitcast.35, f32[6,8,128]{2,1,0:T(8,128)} %copy-done.4, ...), custom_call_target="tpu_custom_call" | custom-call | tf_op jit(solution)/shard_map/pallas_call | solution.py:314
  26.4 0.0 copy-start
  26.4 0.0 copy-start.1
  26.4 0.6 %copy.23 = f32[1,1,3,512]{3,1,2,0:T(1,128)} copy(f32[1,1,3,512]{3,1,2,0:T(1,128)S(1)} %bitcast.21) | data formatting | bytes 12288
  27.0 0.0 all-to-all-done.1
  27.0 0.1 copy-done
  27.1 0.0 copy-done.1
  27.1 1.4 %shard_map.160 = (f32[3,4,128]{2,1,0:T(4,128)}, f32[2]{0:T(128)}) custom-call(s32[1]{0:T(128)} %bitcast.where_ref, s32[1,8]{1,0:T(1,128)} %bitcast.44, f32[64,128]{1,0:T(8,128)S(1)} %bitcast.22, f32[3,4,128]{2,1,0:T(4,128)S(1)} %bitcast.27, f32[3,4,128]{2,1,0:T(4,128)S(1)} %bitcast.29), custom_call_target="tpu_custom_call" | custom-call | tf_op jit(solution)/shard_map/pallas_call | solution.py:318
Async XLA Ops:
  1.5 13.9 %copy-start.2 = (f32[1,1,3,512]{3,1,2,0:T(1,128)S(1)}, f32[1,1,3,512]{3,1,2,0:T(1,128)}, u32[]{:S(2)}) copy-start(f32[1,1,3,512]{3,1,2,0:T(1,128)} %param.17) | copy-start | bytes 18436
  16.5 2.7 %copy-start.3 = (f32[1,1,6,1024]{3,1,2,0:T(1,128)S(1)}, f32[1,1,6,1024]{3,1,2,0:T(1,128)}, u32[]{:S(2)}) copy-start(f32[1,1,6,1024]{3,1,2,0:T(1,128)} %param.18) | copy-start | bytes 73732
  16.5 10.5 %all-to-all-start.1 = ((f32[32,2,128]{2,1,0:T(2,128)}), f32[32,2,128]{2,1,0:T(2,128)S(1)}, u32[]{:S(2)}, u32[]{:S(2)}) async-start(f32[32,2,128]{2,1,0:T(2,128)} %bitcast.18), calls=%async_computation.1 | async-start | bytes 65536 | tf_op jit(solution)/shard_map/all_to_all | solution.py:310
  19.1 4.8 %collective-permute-start = (f32[6,8,128]{2,1,0:T(8,128)S(1)}, f32[6,8,128]{2,1,0:T(8,128)S(1)}, u32[]{:S(2)}, u32[]{:S(2)}) collective-permute-start(f32[6,8,128]{2,1,0:T(8,128)S(1)} %bitcast.36), channel_id=1, source_target_pairs={{0,1},{1,2},{2,3},{3,0},{4,5},{5,6},{6,7},{7,4},{8,9},{9,10},{10,1... | collective-permute-start | bytes 73736 | tf_op jit(solution)/shard_map/ppermute | solution.py:284
  19.3 4.6 %collective-permute-start.1 = (f32[6,8,128]{2,1,0:T(8,128)S(1)}, f32[6,8,128]{2,1,0:T(8,128)S(1)}, u32[]{:S(2)}, u32[]{:S(2)}) collective-permute-start(f32[6,8,128]{2,1,0:T(8,128)S(1)} %bitcast.37), channel_id=1, source_target_pairs={{0,2},{1,3},{2,0},{3,1},{4,6},{5,7},{6,4},{7,5},{8,10},{9,11},{10,... | collective-permute-start | bytes 73736 | tf_op jit(solution)/shard_map/ppermute | solution.py:284
  21.0 3.0 %collective-permute-start.2 = (f32[6,8,128]{2,1,0:T(8,128)S(1)}, f32[6,8,128]{2,1,0:T(8,128)S(1)}, u32[]{:S(2)}, u32[]{:S(2)}) collective-permute-start(f32[6,8,128]{2,1,0:T(8,128)S(1)} %bitcast.38), channel_id=1, source_target_pairs={{0,3},{1,0},{2,1},{3,2},{4,7},{5,4},{6,5},{7,6},{8,11},{9,8},{10,9... | collective-permute-start | bytes 73736 | tf_op jit(solution)/shard_map/ppermute | solution.py:284
  23.9 0.6 %copy-start.4 = (f32[6,8,128]{2,1,0:T(8,128)}, f32[6,8,128]{2,1,0:T(8,128)S(1)}, u32[]{:S(2)}) copy-start(f32[6,8,128]{2,1,0:T(8,128)S(1)} %collective-permute-done.refs_1_) | copy-start | bytes 73732
  24.0 0.6 %copy-start.5 = (f32[6,8,128]{2,1,0:T(8,128)}, f32[6,8,128]{2,1,0:T(8,128)S(1)}, u32[]{:S(2)}) copy-start(f32[6,8,128]{2,1,0:T(8,128)S(1)} %collective-permute-done.1.refs_2_) | copy-start | bytes 73732
  24.0 0.6 %copy-start.6 = (f32[6,8,128]{2,1,0:T(8,128)}, f32[6,8,128]{2,1,0:T(8,128)S(1)}, u32[]{:S(2)}) copy-start(f32[6,8,128]{2,1,0:T(8,128)S(1)} %collective-permute-done.2.refs_3_) | copy-start | bytes 73732
  26.4 0.7 %copy-start = (f32[1,1,3,512]{3,1,2,0:T(1,128)S(1)}, f32[1,1,3,512]{3,1,2,0:T(1,128)}, u32[]{:S(2)}) copy-start(f32[1,1,3,512]{3,1,2,0:T(1,128)} %param.13) | copy-start | bytes 18436
  26.4 0.7 %copy-start.1 = (f32[1,1,3,512]{3,1,2,0:T(1,128)S(1)}, f32[1,1,3,512]{3,1,2,0:T(1,128)}, u32[]{:S(2)}) copy-start(f32[1,1,3,512]{3,1,2,0:T(1,128)} %param.14) | copy-start | bytes 18436

commit v3 on v2

--- a/solution.py
+++ b/solution.py
@@ -76,18 +76,23 @@
     return result
 
 
-def pack_kernel(block, counts_ref, copies_ref, duals_ref, ids_ref, out_ref):
+def pack_kernel(block, counts_ref, copies_ref, duals_ref, ids_ref, out_ref, live_ref):
     rows = ids_ref.shape[0]
     per = LANES // block
     lane = lax.broadcasted_iota(jnp.int32, (rows, LANES), 1)
     sources = [copies_ref[k] for k in range(3)] + [duals_ref[k] for k in range(3)]
     sources.append(ids_ref[...].astype(jnp.float32))
+    mask = jnp.zeros((rows, LANES), jnp.float32)
     for j in range(per):
         for v, source in enumerate(sources):
             moved = pltpu.roll(source, LANES - j * block, 1) if j else source
             out_ref[pl.ds(j * FIELDS + v, rows, per * FIELDS), :] = moved
-        live = (lane < column_of(counts_ref, j, per, rows)).astype(jnp.float32)
+        count = column_of(counts_ref, j, per, rows)
+        live = (lane < count).astype(jnp.float32)
         out_ref[pl.ds(j * FIELDS + 7, rows, per * FIELDS), :] = live
+        here = (lane >= j * block) & (lane < j * block + count)
+        mask = jnp.where(here, 1.0, mask)
+    live_ref[...] = mask
 
 
 def owner_kernel(block, subs, recv_ref, old_ref, consensus_ref, out_ref):
@@ -166,14 +171,14 @@
         out_ref[a] = high + (middle + low)
 
 
-def refine_kernel(where_ref, edge_ref, grad_ref, inverse_ref, offset_ref, *refs):
+def refine_kernel(edge_ref, grad_ref, inverse_ref, offset_ref, *refs):
     blocks, out_ref = refs[:-1], refs[-1]
     pose_ref = blocks[0]
     subs = len(blocks)
     rows = edge_ref.shape[0]
     count = rows * LANES
     edge = edge_ref[...]
-    place = lax.rem(where_ref[0] + subs - edge // count, subs)
+    place = lax.rem(lax.axis_index("sub") + subs - edge // count, subs)
     tables = [
         [held[a, pl.ds(k, 1), :] for held in blocks for k in range(rows)] for a in range(6)
     ]
@@ -187,19 +192,17 @@
 
 
 def finish_kernel(
-    block, subs, landmark_total, where_ref, counts_ref, recv_ref, copies_ref, duals_ref,
-    dual_ref, norm_ref,
+    block, subs, landmark_total, recv_ref, live_ref, copies_ref, duals_ref, dual_ref, norm_ref
 ):
     rows = copies_ref.shape[1]
     per = LANES // block
     robots = rows * per
-    me = where_ref[0]
+    me = lax.axis_index("sub")
     lane = lax.broadcasted_iota(jnp.int32, (rows, LANES), 1)
     back = [jnp.zeros((rows, LANES), jnp.float32) for _ in range(3)]
-    live = jnp.zeros((rows, LANES), jnp.bool_)
+    live = live_ref[...]
     for j in range(per):
         here = (lane >= j * block) & (lane < (j + 1) * block)
-        live = live | (here & (lane - j * block < column_of(counts_ref, j, per, rows)))
         for v, (line, at) in enumerate(((0, 0), (0, block), (1, 0))):
             start = 2 * (j * subs + me) + line
             got = recv_ref[pl.ds(start, rows, 2 * subs * per), :]
@@ -207,8 +210,7 @@
             moved = pltpu.roll(got, turn, 1) if turn else got
             back[v] = jnp.where(here, moved, back[v])
     for v in range(3):
-        differ = jnp.where(live, copies_ref[v] - back[v], 0.0)
-        dual_ref[v] = duals_ref[v] + differ
+        dual_ref[v] = duals_ref[v] + (copies_ref[v] - back[v]) * live
     sums = jnp.sum(recv_ref[pl.ds(1, robots * subs, 2), :], axis=0, keepdims=True)
     norms = jnp.sqrt(sums / landmark_total)
     lane = lax.broadcasted_iota(jnp.int32, (1, LANES), 1)
@@ -277,15 +279,17 @@
     edges = edge_to.reshape(pose_rows, LANES)
     offset = edge_offset.reshape(6, pose_rows, LANES)
 
-    where = lax.axis_index("sub").astype(jnp.int32).reshape(1)
     held = [pose_block]
     for k in range(1, subs):
         ring = [(i, (i + k) % subs) for i in range(subs)]
         held.append(lax.ppermute(pose_block, "sub", ring))
 
-    (outgoing,) = call(
+    outgoing, live = call(
         functools.partial(pack_kernel, block),
-        [pltpu.VMEM((robots * FIELDS, LANES), jnp.float32)],
+        [
+            pltpu.VMEM((robots * FIELDS, LANES), jnp.float32),
+            pltpu.VMEM((rows, LANES), jnp.float32),
+        ],
         [SMEM, VMEM, VMEM, VMEM],
     )(counts, copies, duals, ids)
     received = lax.all_to_all(
@@ -312,15 +316,15 @@
     ).reshape(robots * subs * 2, LANES)
 
     (refined,) = call(
-        refine_kernel, [(6, pose_rows, LANES)], [SMEM] + [VMEM] * (4 + subs)
-    )(where, edges, in_vmem(grad_obs), inverse, offset, *held)
+        refine_kernel, [(6, pose_rows, LANES)], [VMEM] * (4 + subs)
+    )(edges, in_vmem(grad_obs), inverse, offset, *[in_vmem(value) for value in held])
 
     dual_new, residual_norms = call(
         functools.partial(finish_kernel, block, subs, float(owned * robots * subs)),
         [(3, rows, LANES), (2,)],
-        [SMEM, SMEM, VMEM, VMEM, VMEM],
+        [VMEM] * 4,
         out_specs=[VMEM, SMEM],
-    )(where, counts, in_vmem(back), in_vmem(copies), in_vmem(duals))
+    )(in_vmem(back), in_vmem(live), in_vmem(copies), in_vmem(duals))
     return (
         refined.reshape(1, 1, 6, pose_count),
         consensus.reshape(1, 1, 3, owned),

time: 29.1 us -> 28.1 us (0.966)
  waiting for transfers between devices: 0.01 us -> 1.8 us
  starting transfers between devices: 5.82 us -> 4.62 us
  Pallas kernels: 6.74 us -> 6.07 us
  local copies, waits for them, and re-layouts: 1.32 us -> 0.71 us
    ppermute x3, waiting for transfers between devices: 0.01 us -> 1.8 us  [step(): held.append(lax.ppermute(pose_block, 'sub', ring))]
    ppermute x3, starting transfers between devices: 3.17 us -> 1.94 us  [step(): held.append(lax.ppermute(pose_block, 'sub', ring))]
    pallas_call x1, Pallas kernels: 1.37 us -> 0.71 us  [step(): call(functools.partial(finish_kernel, block, subs, float(owned * robots *...]
    unnamed x15 -> x9, local copies, waits for them, and re-layouts: 1.32 us -> 0.71 us
  transfers between devices with their start and end apart: 4 -> 4, of which waited for: 0 -> 1; matrix products, arithmetic and copies ran while one was open for 2% -> 2% of each run, Pallas kernels for 12% -> 12%
where the time goes in v3:
time: 28.1 us; the launch traced here: 27.8 us
  blocking collectives  13.9 us (49%)
  Pallas kernels  6.07 us (22%)
  starting transfers between devices  4.62 us (16%)
  waiting for transfers between devices  1.8 us (6%)
  local copies, waits for them, and re-layouts  0.71 us (3%)
  between operations  0.67 us (2%)
    all_to_all x1, blocking collectives, step(): lax.all_to_all(outgoing.reshape(robots, FIELDS, LANES), 'robot', 0, 0, ti...  13.9 us
    all_to_all x1, starting transfers between devices, step(): lax.all_to_all(returning.reshape(robots * subs, 2, LANES), ('robot', 'sub...  2.68 us
    ppermute x3, starting transfers between devices, step(): held.append(lax.ppermute(pose_block, 'sub', ring))  1.94 us
    pallas_call x1, Pallas kernels, step(): call(refine_kernel, [(6, pose_rows, LANES)], [VMEM] * (4 + subs))  1.82 us
    ppermute x3, waiting for transfers between devices, step(): held.append(lax.ppermute(pose_block, 'sub', ring))  1.8 us
    pallas_call x1, Pallas kernels, step(): call(observe_kernel, [pltpu.VMEM((6, pose_rows, LANES), jnp.float32)], [V...  1.61 us
    pallas_call x1, Pallas kernels, step(): call(functools.partial(owner_kernel, block, subs), [pltpu.VMEM((3, owned_...  1.06 us
    pallas_call x1, Pallas kernels, step(): call(functools.partial(pack_kernel, block), [pltpu.VMEM((robots * FIELDS,...  0.88 us
  transfers between devices with their start and end apart: 4, of which 1 were waited for; matrix products, arithmetic and copies ran while one was open for 2% of the time, Pallas kernels for 12%

profile of v3, /device:TPU:0, one launch (start us, length us, event | category | flops | bytes accessed | tf_op | source)
XLA Modules:
  0.0 27.8 jit_solution(17355998874627651857)
XLA Ops:
  0.6 0.9 %shard_map.158 = (f32[64,128]{1,0:T(8,128)S(1)}, f32[4,128]{1,0:T(4,128)S(1)}) custom-call(s32[1,8]{1,0:T(1,128)} %bitcast.43, f32[3,4,128]{2,1,0:T(4,128)} %bitcast.23, f32[3,4,128]{2,1,0:T(4,128)} %bitcast.31, s32[4,128]{1,0:T(4,128)} %bitcast.42), custom_call_target="tpu_custom_call" | custom-call | tf_op jit(solution)/shard_map/pallas_call | solution.py:287
  1.5 0.0 copy-start.3
  1.5 13.9 %all_to_all.10 = f32[8,8,128]{2,1,0:T(8,128)S(1)} all-to-all(f32[8,8,128]{2,1,0:T(8,128)S(1)} %bitcast.26), channel_id=1, replica_groups=mesh['robot'=8,'sub'=4] {'robot'}, dimensions={0} | all-to-all | bytes 65536 | tf_op jit(solution)/shard_map/all_to_all | solution.py:295
  15.4 0.0 copy-done.3
  15.4 1.1 %shard_map.159 = (f32[3,4,128]{2,1,0:T(4,128)S(1)}, f32[64,128]{1,0:T(8,128)}) custom-call(f32[64,128]{1,0:T(8,128)S(1)} %bitcast.22, f32[3,4,128]{2,1,0:T(4,128)S(1)} %bitcast.33), custom_call_target="tpu_custom_call" | custom-call | tf_op jit(solution)/shard_map/pallas_call | solution.py:306
  16.5 0.0 copy-start.1
  16.5 2.7 %all-to-all-start.1 = ((f32[32,2,128]{2,1,0:T(2,128)}), f32[32,2,128]{2,1,0:T(2,128)S(1)}, u32[]{:S(2)}, u32[]{:S(2)}) async-start(f32[32,2,128]{2,1,0:T(2,128)} %bitcast.17), calls=%async_computation.1 | async-start | bytes 65536 | tf_op jit(solution)/shard_map/all_to_all | solution.py:314
  19.2 0.0 copy-done.1
  19.2 1.4 %collective-permute-start.2 = (f32[6,8,128]{2,1,0:T(8,128)S(1)}, f32[6,8,128]{2,1,0:T(8,128)S(1)}, u32[]{:S(2)}, u32[]{:S(2)}) collective-permute-start(f32[6,8,128]{2,1,0:T(8,128)S(1)} %bitcast.27), channel_id=1, source_target_pairs={{0,3},{1,0},{2,1},{3,2},{4,7},{5,4},{6,5},{7,6},{8,11},{9,8},{10,9... | collective-permute-start | bytes 73736 | tf_op jit(solution)/shard_map/ppermute | solution.py:285
  20.6 0.4 %collective-permute-start.1 = (f32[6,8,128]{2,1,0:T(8,128)S(1)}, f32[6,8,128]{2,1,0:T(8,128)S(1)}, u32[]{:S(2)}, u32[]{:S(2)}) collective-permute-start(f32[6,8,128]{2,1,0:T(8,128)S(1)} %bitcast.28), channel_id=1, source_target_pairs={{0,2},{1,3},{2,0},{3,1},{4,6},{5,7},{6,4},{7,5},{8,10},{9,11},{10,... | collective-permute-start | bytes 73736 | tf_op jit(solution)/shard_map/ppermute | solution.py:285
  21.0 0.1 collective-permute-start
  21.1 1.6 %shard_map.156.grad_ref = f32[6,8,128]{2,1,0:T(8,128)S(1)} custom-call(f32[3,4,128]{2,1,0:T(4,128)} %bitcast.24, f32[3,32,128]{2,1,0:T(8,128)} %bitcast.36, f32[18,32,128]{2,1,0:T(8,128)} %bitcast.34, s32[32,128]{1,0:T(8,128)} %bitcast.39, s32[32,128]{1,0:T(8,128)} %bitcast.40), custom_call_target="tpu_custom_call" | custom-call | tf_op jit(solution)/shard_map/pallas_call | solution.py:299
  22.7 0.0 collective-permute-done.2.refs_3_
  22.7 1.8 %collective-permute-done.1.refs_2_ = f32[6,8,128]{2,1,0:T(8,128)S(1)} collective-permute-done((f32[6,8,128]{2,1,0:T(8,128)S(1)}, f32[6,8,128]{2,1,0:T(8,128)S(1)}, u32[]{:S(2)}, u32[]{:S(2)}) %collective-permute-start.1) | collective-permute-done | bytes 24608 | tf_op jit(solution)/shard_map/ppermute | solution.py:285
  24.5 0.0 collective-permute-done.refs_1_
  24.5 1.8 %shard_map.157 = f32[6,8,128]{2,1,0:T(8,128)} custom-call(s32[8,128]{1,0:T(8,128)} %bitcast.41, f32[6,8,128]{2,1,0:T(8,128)S(1)} %shard_map.156.grad_ref, f32[36,8,128]{2,1,0:T(8,128)} %bitcast.35, f32[6,8,128]{2,1,0:T(8,128)} %bitcast.37, f32[6,8,128]{2,1,0:T(8,128)S(1)} %bitcast.30, f32[6,8,128]{2,1,0:T(8,128)S(1)} %collective-permute-done.refs_1_, ...), custom_call_target="tpu_custom_call" | custom-call | tf_op jit(solution)/shard_map/pallas_call | solution.py:318
  26.3 0.0 copy-start
  26.3 0.0 copy-start.2
  26.3 0.6 %copy.23 = f32[1,1,3,512]{3,1,2,0:T(1,128)} copy(f32[1,1,3,512]{3,1,2,0:T(1,128)S(1)} %bitcast.20) | data formatting | bytes 12288
  26.9 0.0 all-to-all-done.1
  26.9 0.1 copy-done
  27.0 0.0 copy-done.2
  27.1 0.7 %shard_map.160 = (f32[3,4,128]{2,1,0:T(4,128)}, f32[2]{0:T(128)}) custom-call(f32[64,128]{1,0:T(8,128)S(1)} %bitcast.21, f32[4,128]{1,0:T(4,128)S(1)} %get-tuple-element.13.live_ref, f32[3,4,128]{2,1,0:T(4,128)S(1)} %bitcast.25, f32[3,4,128]{2,1,0:T(4,128)S(1)} %bitcast.32), custom_call_target="tpu_custom_call" | custom-call | tf_op jit(solution)/shard_map/pallas_call | solution.py:322
Async XLA Ops:
  1.5 13.9 %copy-start.3 = (f32[1,1,3,512]{3,1,2,0:T(1,128)S(1)}, f32[1,1,3,512]{3,1,2,0:T(1,128)}, u32[]{:S(2)}) copy-start(f32[1,1,3,512]{3,1,2,0:T(1,128)} %param.17) | copy-start | bytes 18436
  16.5 2.7 %copy-start.1 = (f32[1,1,6,1024]{3,1,2,0:T(1,128)S(1)}, f32[1,1,6,1024]{3,1,2,0:T(1,128)}, u32[]{:S(2)}) copy-start(f32[1,1,6,1024]{3,1,2,0:T(1,128)} %param.18) | copy-start | bytes 73732
  16.5 10.5 %all-to-all-start.1 = ((f32[32,2,128]{2,1,0:T(2,128)}), f32[32,2,128]{2,1,0:T(2,128)S(1)}, u32[]{:S(2)}, u32[]{:S(2)}) async-start(f32[32,2,128]{2,1,0:T(2,128)} %bitcast.17), calls=%async_computation.1 | async-start | bytes 65536 | tf_op jit(solution)/shard_map/all_to_all | solution.py:314
  19.2 3.6 %collective-permute-start.2 = (f32[6,8,128]{2,1,0:T(8,128)S(1)}, f32[6,8,128]{2,1,0:T(8,128)S(1)}, u32[]{:S(2)}, u32[]{:S(2)}) collective-permute-start(f32[6,8,128]{2,1,0:T(8,128)S(1)} %bitcast.27), channel_id=1, source_target_pairs={{0,3},{1,0},{2,1},{3,2},{4,7},{5,4},{6,5},{7,6},{8,11},{9,8},{10,9... | collective-permute-start | bytes 73736 | tf_op jit(solution)/shard_map/ppermute | solution.py:285
  20.6 3.9 %collective-permute-start.1 = (f32[6,8,128]{2,1,0:T(8,128)S(1)}, f32[6,8,128]{2,1,0:T(8,128)S(1)}, u32[]{:S(2)}, u32[]{:S(2)}) collective-permute-start(f32[6,8,128]{2,1,0:T(8,128)S(1)} %bitcast.28), channel_id=1, source_target_pairs={{0,2},{1,3},{2,0},{3,1},{4,6},{5,7},{6,4},{7,5},{8,10},{9,11},{10,... | collective-permute-start | bytes 73736 | tf_op jit(solution)/shard_map/ppermute | solution.py:285
  21.0 3.6 %collective-permute-start = (f32[6,8,128]{2,1,0:T(8,128)S(1)}, f32[6,8,128]{2,1,0:T(8,128)S(1)}, u32[]{:S(2)}, u32[]{:S(2)}) collective-permute-start(f32[6,8,128]{2,1,0:T(8,128)S(1)} %bitcast.29), channel_id=1, source_target_pairs={{0,1},{1,2},{2,3},{3,0},{4,5},{5,6},{6,7},{7,4},{8,9},{9,10},{10,1... | collective-permute-start | bytes 73736 | tf_op jit(solution)/shard_map/ppermute | solution.py:285
  26.3 0.7 %copy-start = (f32[1,1,3,512]{3,1,2,0:T(1,128)S(1)}, f32[1,1,3,512]{3,1,2,0:T(1,128)}, u32[]{:S(2)}) copy-start(f32[1,1,3,512]{3,1,2,0:T(1,128)} %param.13) | copy-start | bytes 18436
  26.3 0.7 %copy-start.2 = (f32[1,1,3,512]{3,1,2,0:T(1,128)S(1)}, f32[1,1,3,512]{3,1,2,0:T(1,128)}, u32[]{:S(2)}) copy-start(f32[1,1,3,512]{3,1,2,0:T(1,128)} %param.14) | copy-start | bytes 18436

commit v4 on v3

--- a/solution.py
+++ b/solution.py
@@ -13,6 +13,7 @@
 SUBLANES = 8
 FIELDS = 8
 SHIFT = LANES.bit_length() - 1
+WHOLE_BYTES = 2 << 20
 
 
 def split3(value):
@@ -76,7 +77,98 @@
     return result
 
 
-def pack_kernel(block, counts_ref, copies_ref, duals_ref, ids_ref, out_ref, live_ref):
+def slot_sums(field, live, ids, out_rows):
+    pieces = [split3(live * (field[v] + field[3 + v])) for v in range(3)]
+    planes = [pieces[v][s] for s in range(3) for v in range(3)] + [live]
+    sums = segment_rows(
+        lambda t: [plane[t : t + 1] for plane in planes],
+        lambda t: ids[t : t + 1],
+        ids.shape[0],
+        out_rows,
+    )
+    part = [sums[j * out_rows : (j + 1) * out_rows] for j in range(10)]
+    return [part[v] + (part[3 + v] + part[6 + v]) for v in range(3)] + [part[9]]
+
+
+def write_sending(pose_ref, primal, dual, out_ref):
+    rows = pose_ref.shape[1]
+    for a in range(6):
+        out_ref[pl.ds(a * rows, rows), :] = pose_ref[a]
+    primal = jnp.sum(primal, axis=0, keepdims=True)
+    dual = penalty * penalty * jnp.sum(dual, axis=0, keepdims=True)
+    sub = lax.broadcasted_iota(jnp.int32, (SUBLANES, LANES), 0)
+    out_ref[pl.ds(6 * rows, SUBLANES), :] = jnp.where(
+        sub == 0, primal, jnp.where(sub == 1, dual, 0.0)
+    )
+
+
+def block_rows(rows, owned_rows):
+    used = FIELDS * rows + 3 * owned_rows
+    return -(-used // SUBLANES) * SUBLANES
+
+
+def pack_kernel(block, counts_ref, copies_ref, duals_ref, ids_ref, old_ref, out_ref, live_ref):
+    rows, owned_rows = ids_ref.shape[0], old_ref.shape[1]
+    height = block_rows(rows, owned_rows)
+    per = LANES // block
+    lane = lax.broadcasted_iota(jnp.int32, (rows, LANES), 1)
+    live = jnp.zeros((rows, LANES), jnp.float32)
+    for j in range(per):
+        count = column_of(counts_ref, j, per, rows)
+        live = jnp.where((lane >= j * block) & (lane < j * block + count), 1.0, live)
+    live_ref[...] = live
+    planes = [copies_ref[k] for k in range(3)] + [duals_ref[k] for k in range(3)]
+    planes += [ids_ref[...].astype(jnp.float32), live] + [old_ref[k] for k in range(3)]
+    used = FIELDS * rows + 3 * owned_rows
+    if height > used:
+        planes.append(jnp.zeros((height - used, LANES), jnp.float32))
+    whole = jnp.concatenate(planes, axis=0)
+    for d in range(out_ref.shape[0] // height):
+        out_ref[pl.ds(d * height, height), :] = whole
+
+
+def consensus_kernel(
+    block, owned_rows, recv_ref, pose_ref, out_ref, back_ref, consensus_ref, backs_ref, news_ref
+):
+    rows = back_ref.shape[1]
+    height = block_rows(rows, owned_rows)
+    robots = recv_ref.shape[0] // height
+    per = LANES // block
+    wide = per * owned_rows
+    side = lax.broadcasted_iota(jnp.int32, (robots, LANES), 1) // block * (owned_rows * LANES)
+    primal = jnp.zeros((robots, LANES), jnp.float32)
+    dual = jnp.zeros((wide, LANES), jnp.float32)
+    for k in range(rows):
+        field = [recv_ref[pl.ds(v * rows + k, robots, height), :] for v in range(FIELDS)]
+        live = field[7]
+        ids = field[6].astype(jnp.int32) + side
+        sums = slot_sums(field, live, ids, wide)
+        tables = []
+        for v in range(3):
+            start = FIELDS * rows + v * owned_rows
+            lines = [
+                recv_ref[pl.ds((k * per + j) * height + start, owned_rows), :] for j in range(per)
+            ]
+            old = jnp.concatenate(lines, axis=0)
+            new = (old + sums[v]) / (1.0 + sums[3])
+            for j in range(per):
+                news_ref[v, k * per + j] = new[j * owned_rows : (j + 1) * owned_rows]
+            change = new - old
+            dual = dual + sums[3] * change * change
+            tables.append([new[j : j + 1] for j in range(wide)])
+        back = lookup(tables, ids, robots)
+        for v in range(3):
+            backs_ref[v, pl.ds(k * robots, robots), :] = back[v]
+            differ = (field[v] - back[v]) * live
+            primal = primal + differ * differ
+    me = lax.axis_index("robot")
+    for v in range(3):
+        back_ref[v] = backs_ref[v, pl.ds(me, rows, robots), :]
+        consensus_ref[v] = news_ref[v, me]
+    write_sending(pose_ref, primal, dual, out_ref)
+
+
+def pack_blocks_kernel(block, counts_ref, copies_ref, duals_ref, ids_ref, out_ref, live_ref):
     rows = ids_ref.shape[0]
     per = LANES // block
     lane = lax.broadcasted_iota(jnp.int32, (rows, LANES), 1)
@@ -95,35 +187,22 @@
     live_ref[...] = mask
 
 
-def owner_kernel(block, subs, recv_ref, old_ref, consensus_ref, out_ref):
+def owner_kernel(block, recv_ref, old_ref, consensus_ref, out_ref):
     robots = recv_ref.shape[0] // FIELDS
     rows = old_ref.shape[1]
-    padded = max(rows, SUBLANES)
     field = [recv_ref[pl.ds(v, robots, FIELDS), :] for v in range(FIELDS)]
     live = field[7]
     ids = field[6].astype(jnp.int32)
-    pieces = [split3(live * (field[v] + field[3 + v])) for v in range(3)]
-    planes = [pieces[v][s] for s in range(3) for v in range(3)] + [live]
-    sums = segment_rows(
-        lambda t: [plane[t : t + 1] for plane in planes],
-        lambda t: ids[t : t + 1],
-        robots,
-        padded,
-    )
-
-    def plane_sum(j):
-        return sums[j * padded : j * padded + rows]
-
-    seen = plane_sum(9)
-    weight = 1.0 + seen
-    dual_sum = jnp.zeros((rows, LANES), jnp.float32)
+    sums = slot_sums(field, live, ids, max(rows, SUBLANES))
+    seen = sums[3][:rows]
+    dual = jnp.zeros((rows, LANES), jnp.float32)
     tables = []
     for v in range(3):
         old = old_ref[v]
-        new = (old + (plane_sum(v) + (plane_sum(3 + v) + plane_sum(6 + v)))) / weight
+        new = (old + sums[v][:rows]) / (1.0 + seen)
         consensus_ref[v] = new
         change = new - old
-        dual_sum = dual_sum + seen * change * change
+        dual = dual + seen * change * change
         tables.append([new[k : k + 1] for k in range(rows)])
     back = lookup(tables, ids, robots)
     primal = jnp.zeros((robots, LANES), jnp.float32)
@@ -131,17 +210,42 @@
         differ = (field[v] - back[v]) * live
         primal = primal + differ * differ
     primal = jnp.sum(primal, axis=(0, 1), keepdims=True)
-    dual_sum = penalty * penalty * jnp.sum(dual_sum, axis=(0, 1), keepdims=True)
+    dual = jnp.sum(dual, axis=(0, 1), keepdims=True)
     lane = lax.broadcasted_iota(jnp.int32, (robots, LANES), 1)
+    partial = jnp.where(lane == block, primal, jnp.where(lane == block + 1, dual, 0.0))
     first = jnp.where(lane < block, back[0], pltpu.roll(back[1], block, 1))
-    sums_row = jnp.where(lane == block, primal, jnp.where(lane == block + 1, dual_sum, 0.0))
-    second = jnp.where(lane < block, back[2], sums_row)
-    for s in range(subs):
-        out_ref[pl.ds(2 * s, robots, 2 * subs), :] = first
-        out_ref[pl.ds(2 * s + 1, robots, 2 * subs), :] = second
-
-
-def observe_kernel(copies_ref, measured_ref, jac_ref, slot_ref, pose_ref, out_ref, planes_ref):
+    out_ref[pl.ds(0, robots, 2), :] = first
+    out_ref[pl.ds(1, robots, 2), :] = jnp.where(lane < block, back[2], partial)
+
+
+def collect_kernel(block, recv_ref, pose_ref, out_ref, back_ref):
+    rows = back_ref.shape[1]
+    per = LANES // block
+    lane = lax.broadcasted_iota(jnp.int32, (rows, LANES), 1)
+    back = [jnp.zeros((rows, LANES), jnp.float32) for _ in range(3)]
+    for j in range(per):
+        here = (lane >= j * block) & (lane < (j + 1) * block)
+        for v, (line, at) in enumerate(((0, 0), (0, block), (1, 0))):
+            got = recv_ref[pl.ds(2 * j + line, rows, 2 * per), :]
+            turn = (j * block - at) % LANES
+            moved = pltpu.roll(got, turn, 1) if turn else got
+            back[v] = jnp.where(here, moved, back[v])
+    for v in range(3):
+        back_ref[v] = back[v]
+    partial = recv_ref[pl.ds(1, rows * per, 2), :]
+    lane = lax.broadcasted_iota(jnp.int32, partial.shape, 1)
+    primal = jnp.where(lane == block, partial, 0.0)
+    dual = jnp.where(lane == block + 1, partial, 0.0)
+    write_sending(pose_ref, primal, dual, out_ref)
+
+
+def observe_kernel(
+    copies_ref, measured_ref, jac_ref, slot_ref, pose_ref, duals_ref, live_ref, back_ref,
+    estimate_ref, out_ref, dual_ref, consensus_ref, planes_ref,
+):
+    for v in range(3):
+        consensus_ref[v] = estimate_ref[v]
+        dual_ref[v] = duals_ref[v] + (copies_ref[v] - back_ref[v]) * live_ref[...]
     rows = slot_ref.shape[0]
     table_rows = copies_ref.shape[1]
     out_rows = out_ref.shape[1]
@@ -171,55 +275,49 @@
         out_ref[a] = high + (middle + low)
 
 
-def refine_kernel(edge_ref, grad_ref, inverse_ref, offset_ref, *refs):
-    blocks, out_ref = refs[:-1], refs[-1]
-    pose_ref = blocks[0]
+def refine_kernel(landmark_total, edge_ref, grad_ref, inverse_ref, offset_ref, *refs):
+    blocks, (out_ref, norm_ref) = refs[:-2], refs[-2:]
     subs = len(blocks)
     rows = edge_ref.shape[0]
     count = rows * LANES
+    me = lax.axis_index("sub")
     edge = edge_ref[...]
-    place = lax.rem(lax.axis_index("sub") + subs - edge // count, subs)
+    place = lax.rem(me + subs - edge // count, subs)
     tables = [
-        [held[a, pl.ds(k, 1), :] for held in blocks for k in range(rows)] for a in range(6)
+        [held[pl.ds(a * rows + k, 1), :] for held in blocks for k in range(rows)]
+        for a in range(6)
     ]
     far = lookup(tables, place * count + lax.rem(edge, count), rows)
-    grad = [grad_ref[a] + far[a] - pose_ref[a] - offset_ref[a] for a in range(6)]
+    own = [blocks[0][pl.ds(a * rows, rows), :] for a in range(6)]
+    grad = [grad_ref[a] + far[a] - own[a] - offset_ref[a] for a in range(6)]
     for a in range(6):
         delta = inverse_ref[a * 6] * grad[0]
         for b in range(1, 6):
             delta = delta + inverse_ref[a * 6 + b] * grad[b]
-        out_ref[a] = pose_ref[a] + delta
-
-
-def finish_kernel(
-    block, subs, landmark_total, recv_ref, live_ref, copies_ref, duals_ref, dual_ref, norm_ref
-):
-    rows = copies_ref.shape[1]
-    per = LANES // block
-    robots = rows * per
-    me = lax.axis_index("sub")
-    lane = lax.broadcasted_iota(jnp.int32, (rows, LANES), 1)
-    back = [jnp.zeros((rows, LANES), jnp.float32) for _ in range(3)]
-    live = live_ref[...]
-    for j in range(per):
-        here = (lane >= j * block) & (lane < (j + 1) * block)
-        for v, (line, at) in enumerate(((0, 0), (0, block), (1, 0))):
-            start = 2 * (j * subs + me) + line
-            got = recv_ref[pl.ds(start, rows, 2 * subs * per), :]
-            turn = (j * block - at) % LANES
-            moved = pltpu.roll(got, turn, 1) if turn else got
-            back[v] = jnp.where(here, moved, back[v])
-    for v in range(3):
-        dual_ref[v] = duals_ref[v] + (copies_ref[v] - back[v]) * live
-    sums = jnp.sum(recv_ref[pl.ds(1, robots * subs, 2), :], axis=0, keepdims=True)
-    norms = jnp.sqrt(sums / landmark_total)
-    lane = lax.broadcasted_iota(jnp.int32, (1, LANES), 1)
+        out_ref[a] = own[a] + delta
+    total = None
+    for s in range(subs):
+        place = lax.rem(me + subs - s, subs)
+        part = blocks[0][pl.ds(6 * rows, SUBLANES), :]
+        for k in range(1, subs):
+            part = jnp.where(place == k, blocks[k][pl.ds(6 * rows, SUBLANES), :], part)
+        total = part if total is None else total + part
+    norms = jnp.sqrt(jnp.sum(total, axis=1, keepdims=True) / landmark_total)
     for k in range(2):
-        norm_ref[k] = jnp.sum(jnp.where(lane == block + k, norms, 0.0))
+        norm_ref[k] = norms[k, 0]
 
 
 VMEM = pl.BlockSpec(memory_space=pltpu.VMEM)
 SMEM = pl.BlockSpec(memory_space=pltpu.SMEM)
+
+
+def vmem(*shape):
+    return pltpu.VMEM(shape, jnp.float32)
+
+
+def over_robots(value, robots):
+    blocks = value.reshape(robots, value.shape[0] // robots, LANES)
+    return lax.all_to_all(blocks, "robot", 0, 0, tiled=True).reshape(value.shape)
 
 
 def in_vmem(value):
@@ -279,52 +377,73 @@
     edges = edge_to.reshape(pose_rows, LANES)
     offset = edge_offset.reshape(6, pose_rows, LANES)
 
-    held = [pose_block]
+    height = block_rows(rows, owned_rows)
+    sending_rows = 6 * pose_rows + SUBLANES
+    if robots * height * LANES * 4 <= WHOLE_BYTES:
+        outgoing, live = call(
+            functools.partial(pack_kernel, block),
+            [vmem(robots * height, LANES), vmem(rows, LANES)],
+            [SMEM, VMEM, VMEM, VMEM, VMEM],
+        )(counts, copies, duals, ids, old)
+        received = over_robots(outgoing, robots)
+        sending, back, estimate = call(
+            functools.partial(consensus_kernel, block, owned_rows),
+            [vmem(sending_rows, LANES), vmem(3, rows, LANES), vmem(3, owned_rows, LANES)],
+            [VMEM] * 2,
+            scratch=[vmem(3, rows * robots, LANES), vmem(3, robots, owned_rows, LANES)],
+        )(in_vmem(received), in_vmem(pose_block))
+    else:
+        outgoing, live = call(
+            functools.partial(pack_blocks_kernel, block),
+            [vmem(robots * FIELDS, LANES), vmem(rows, LANES)],
+            [SMEM, VMEM, VMEM, VMEM],
+        )(counts, copies, duals, ids)
+        received = over_robots(outgoing, robots)
+        estimate, returning = call(
+            functools.partial(owner_kernel, block),
+            [vmem(3, owned_rows, LANES), vmem(robots * 2, LANES)],
+            [VMEM] * 2,
+        )(in_vmem(received), in_vmem(old))
+        sending, back = call(
+            functools.partial(collect_kernel, block),
+            [vmem(sending_rows, LANES), vmem(3, rows, LANES)],
+            [VMEM] * 2,
+        )(in_vmem(over_robots(returning, robots)), in_vmem(pose_block))
+
+    held = [sending]
     for k in range(1, subs):
         ring = [(i, (i + k) % subs) for i in range(subs)]
-        held.append(lax.ppermute(pose_block, "sub", ring))
-
-    outgoing, live = call(
-        functools.partial(pack_kernel, block),
-        [
-            pltpu.VMEM((robots * FIELDS, LANES), jnp.float32),
-            pltpu.VMEM((rows, LANES), jnp.float32),
-        ],
-        [SMEM, VMEM, VMEM, VMEM],
-    )(counts, copies, duals, ids)
-    received = lax.all_to_all(
-        outgoing.reshape(robots, FIELDS, LANES), "robot", 0, 0, tiled=True
-    ).reshape(robots * FIELDS, LANES)
-
-    (grad_obs,) = call(
+        held.append(lax.ppermute(sending, "sub", ring))
+
+    grad_obs, dual_new, consensus = call(
         observe_kernel,
-        [pltpu.VMEM((6, pose_rows, LANES), jnp.float32)],
-        [VMEM] * 5,
+        [vmem(6, pose_rows, LANES), (3, rows, LANES), (3, owned_rows, LANES)],
+        [VMEM] * 9,
         scratch=[pltpu.VMEM((18, obs_rows, LANES), jnp.float32)],
-    )(copies, measured, jac, slot_ids, pose_ids)
-
-    consensus, returning = call(
-        functools.partial(owner_kernel, block, subs),
-        [
-            pltpu.VMEM((3, owned_rows, LANES), jnp.float32),
-            pltpu.VMEM((robots * subs * 2, LANES), jnp.float32),
-        ],
-        [VMEM, VMEM],
-    )(in_vmem(received), in_vmem(old))
-    back = lax.all_to_all(
-        returning.reshape(robots * subs, 2, LANES), ("robot", "sub"), 0, 0, tiled=True
-    ).reshape(robots * subs * 2, LANES)
-
-    (refined,) = call(
-        refine_kernel, [(6, pose_rows, LANES)], [VMEM] * (4 + subs)
-    )(edges, in_vmem(grad_obs), inverse, offset, *[in_vmem(value) for value in held])
-
-    dual_new, residual_norms = call(
-        functools.partial(finish_kernel, block, subs, float(owned * robots * subs)),
-        [(3, rows, LANES), (2,)],
-        [VMEM] * 4,
+    )(
+        in_vmem(copies),
+        in_vmem(measured),
+        in_vmem(jac),
+        in_vmem(slot_ids),
+        in_vmem(pose_ids),
+        in_vmem(duals),
+        in_vmem(live),
+        in_vmem(back),
+        in_vmem(estimate),
+    )
+
+    refined, residual_norms = call(
+        functools.partial(refine_kernel, float(owned * robots * subs)),
+        [(6, pose_rows, LANES), (2,)],
+        [VMEM] * (4 + subs),
         out_specs=[VMEM, SMEM],
-    )(in_vmem(back), in_vmem(live), in_vmem(copies), in_vmem(duals))
+    )(
+        in_vmem(edges),
+        in_vmem(grad_obs),
+        in_vmem(inverse),
+        in_vmem(offset),
+        *[in_vmem(value) for value in held],
+    )
     return (
         refined.reshape(1, 1, 6, pose_count),
         consensus.reshape(1, 1, 3, owned),

time: 28.1 us -> 23.5 us (0.84)
  starting transfers between devices: 4.62 us -> 1.79 us
  Pallas kernels: 6.07 us -> 3.46 us
  blocking collectives: 13.9 us -> 15.2 us
  waiting for transfers between devices: 1.8 us -> 1.37 us
    all_to_all x1 -> x0, starting transfers between devices: 2.68 us -> none  [step(): lax.all_to_all(returning.reshape(robots * subs, 2, LANES), ('robot', 'sub...]
    pallas_call x5 -> x4, Pallas kernels: 6.07 us -> 3.46 us  [the longest x1 1.06 us: step(): call(observe_kernel, [vmem(6, pose_rows, LANES), (3, rows, LANES), (3, ow...]
    all_to_all x1, blocking collectives: 13.9 us -> 15.2 us  [over_robots(): lax.all_to_all(blocks, 'robot', 0, 0, tiled=True).reshape(value.shape)]
    ppermute x3, waiting for transfers between devices: 1.8 us -> 1.37 us  [step(): held.append(lax.ppermute(sending, 'sub', ring))]
    unnamed x9 -> x20, local copies, waits for them, and re-layouts: 0.71 us -> 0.71 us
  transfers between devices with their start and end apart: 4 -> 3, of which waited for: 1 -> 2; matrix products, arithmetic and copies ran while one was open for 2% -> 0% of each run, Pallas kernels for 12% -> 5%
where the time goes in v4:
time: 23.5 us; the launch traced here: 23.2 us
  blocking collectives  15.2 us (65%)
  Pallas kernels  3.46 us (15%)
  starting transfers between devices  1.79 us (8%)
  waiting for transfers between devices  1.37 us (6%)
  local copies, waits for them, and re-layouts  0.71 us (3%)
  between operations  0.71 us (3%)
    all_to_all x1, blocking collectives, over_robots(): lax.all_to_all(blocks, 'robot', 0, 0, tiled=True).reshape(value.shape)  15.2 us
    ppermute x3, starting transfers between devices, step(): held.append(lax.ppermute(sending, 'sub', ring))  1.79 us
    ppermute x3, waiting for transfers between devices, step(): held.append(lax.ppermute(sending, 'sub', ring))  1.37 us
    pallas_call x1, Pallas kernels, step(): call(observe_kernel, [vmem(6, pose_rows, LANES), (3, rows, LANES), (3, ow...  1.06 us
    pallas_call x1, Pallas kernels, step(): call(functools.partial(refine_kernel, float(owned * robots * subs)), [(6,...  0.95 us
    pallas_call x1, Pallas kernels, step(): call(functools.partial(pack_kernel, block), [vmem(robots * height, LANES)...  0.82 us
    unnamed x20, local copies, waits for them, and re-layouts  0.71 us
    pallas_call x1, Pallas kernels, step(): call(functools.partial(consensus_kernel, block, owned_rows), [vmem(sendin...  0.64 us
  transfers between devices with their start and end apart: 3, of which 2 were waited for; matrix products, arithmetic and copies ran while one was open for 0% of the time, Pallas kernels for 5%

profile of v4, /device:TPU:0, one launch (start us, length us, event | category | flops | bytes accessed | tf_op | source)
XLA Modules:
  0.0 23.2 jit_solution(8335110459479475278)
XLA Ops:
  0.6 0.8 %shard_map.156 = (f32[384,128]{1,0:T(8,128)S(1)}, f32[4,128]{1,0:T(4,128)S(1)}) custom-call(s32[1,8]{1,0:T(1,128)} %bitcast.34, f32[3,4,128]{2,1,0:T(4,128)} %bitcast.25, f32[3,4,128]{2,1,0:T(4,128)} %bitcast.27, s32[4,128]{1,0:T(4,128)} %bitcast.33, f32[3,4,128]{2,1,0:T(4,128)} %bitcast.32), custom_call_target="tpu_custom_call" | custom-call | tf_op jit(solution)/shard_map/pallas_call | solution.py:383
  1.5 0.0 copy-start.3
  1.5 0.0 copy-start
  1.5 15.2 %all_to_all.5 = f32[8,48,128]{2,1,0:T(8,128)S(1)} all-to-all(f32[8,48,128]{2,1,0:T(8,128)S(1)} %bitcast.20), channel_id=1, replica_groups=mesh['robot'=8,'sub'=4] {'robot'}, dimensions={0} | all-to-all | bytes 393216 | tf_op jit(solution)/shard_map/all_to_all | solution.py:320
  16.6 0.0 copy-done.3
  16.7 0.0 copy-start.2
  16.7 0.0 copy-start.7
  16.7 0.0 copy-start.8
  16.7 0.6 %shard_map.157 = (f32[56,128]{1,0:T(8,128)S(1)}, f32[3,4,128]{2,1,0:T(4,128)S(1)}, f32[3,4,128]{2,1,0:T(4,128)S(1)}) custom-call(f32[384,128]{1,0:T(8,128)S(1)} %bitcast.18, f32[6,8,128]{2,1,0:T(8,128)S(1)} %bitcast.23), custom_call_target="tpu_custom_call" | custom-call | tf_op jit(solution)/shard_map/pallas_call | solution.py:389
  17.3 0.1 collective-permute-start.2
  17.4 1.6 %collective-permute-start.1 = (f32[56,128]{1,0:T(8,128)S(1)}, f32[56,128]{1,0:T(8,128)S(1)}, u32[]{:S(2)}, u32[]{:S(2)}) collective-permute-start(f32[56,128]{1,0:T(8,128)S(1)} %get-tuple-element.19.refs_0_), channel_id=1, source_target_pairs={{0,2},{1,3},{2,0},{3,1},{4,6},{5,7},{6,4},{7,5},{8,10},{9,11},{10,... | collective-permute-start | bytes 86024 | tf_op jit(solution)/shard_map/ppermute | solution.py:416
  19.0 0.2 collective-permute-start
  19.1 0.0 copy-start.6
  19.1 0.0 copy-start.5
  19.1 0.0 copy-done
  19.1 0.0 copy-done.2
  19.1 0.0 copy-done.7
  19.1 0.0 copy-done.8
  19.1 0.7 %copy-done.6 = f32[1,1,3,512]{3,1,2,0:T(1,128)S(1)} copy-done((f32[1,1,3,512]{3,1,2,0:T(1,128)S(1)}, f32[1,1,3,512]{3,1,2,0:T(1,128)}, u32[]{:S(2)}) %copy-start.6) | copy-done | bytes 6168
  19.8 0.0 copy-done.5
  19.8 0.0 copy-start.1
  19.8 0.0 copy-start.4
  19.8 1.1 %shard_map.158 = (f32[6,8,128]{2,1,0:T(8,128)S(1)}, f32[3,4,128]{2,1,0:T(4,128)}, f32[3,4,128]{2,1,0:T(4,128)}) custom-call(f32[3,4,128]{2,1,0:T(4,128)S(1)} %bitcast.26, f32[3,32,128]{2,1,0:T(8,128)S(1)} %bitcast.22, f32[18,32,128]{2,1,0:T(8,128)S(1)} %bitcast.19, s32[32,128]{1,0:T(8,128)S(1)} %bitcast.29, s32[32,128]{1,0:T(8,128)S(1)} %bitcast.30, ...), custom_call_target="tpu_custom_call" | custom-call | tf_op jit(solution)/shard_map/pallas_call | solution.py:418
  20.9 0.0 copy-start.9
  20.9 0.0 collective-permute-done.2.refs_3_
  20.9 0.5 %collective-permute-done.1.refs_2_ = f32[56,128]{1,0:T(8,128)S(1)} collective-permute-done((f32[56,128]{1,0:T(8,128)S(1)}, f32[56,128]{1,0:T(8,128)S(1)}, u32[]{:S(2)}, u32[]{:S(2)}) %collective-permute-start.1) | collective-permute-done | bytes 28704 | tf_op jit(solution)/shard_map/ppermute | solution.py:416
  21.3 0.9 %collective-permute-done.refs_1_ = f32[56,128]{1,0:T(8,128)S(1)} collective-permute-done((f32[56,128]{1,0:T(8,128)S(1)}, f32[56,128]{1,0:T(8,128)S(1)}, u32[]{:S(2)}, u32[]{:S(2)}) %collective-permute-start) | collective-permute-done | bytes 28704 | tf_op jit(solution)/shard_map/ppermute | solution.py:416
  22.2 0.0 copy-done.1
  22.3 0.0 copy-done.4
  22.3 0.0 copy-done.9
  22.3 0.9 %shard_map.159 = (f32[6,8,128]{2,1,0:T(8,128)}, f32[2]{0:T(128)}) custom-call(s32[8,128]{1,0:T(8,128)S(1)} %bitcast.31, f32[6,8,128]{2,1,0:T(8,128)S(1)} %get-tuple-element.18.grad_ref, f32[36,8,128]{2,1,0:T(8,128)S(1)} %bitcast.21, f32[6,8,128]{2,1,0:T(8,128)S(1)} %bitcast.24, f32[56,128]{1,0:T(8,128)S(1)} %get-tuple-element.19.refs_0_, ...), custom_call_target="tpu_custom_call" | custom-call | tf_op jit(solution)/shard_map/pallas_call | solution.py:435
Async XLA Ops:
  1.5 15.2 %copy-start.3 = (f32[1,1,6,1024]{3,1,2,0:T(1,128)S(1)}, f32[1,1,6,1024]{3,1,2,0:T(1,128)}, u32[]{:S(2)}) copy-start(f32[1,1,6,1024]{3,1,2,0:T(1,128)} %param.18) | copy-start | bytes 73732
  1.5 17.6 %copy-start = (f32[1,1,18,4096]{3,1,2,0:T(1,128)S(1)}, f32[1,1,18,4096]{3,1,2,0:T(1,128)}, u32[]{:S(2)}) copy-start(f32[1,1,18,4096]{3,1,2,0:T(1,128)} %param.20) | copy-start | bytes 884740
  16.7 2.5 %copy-start.2 = (f32[1,1,3,4096]{3,1,2,0:T(1,128)S(1)}, f32[1,1,3,4096]{3,1,2,0:T(1,128)}, u32[]{:S(2)}) copy-start(f32[1,1,3,4096]{3,1,2,0:T(1,128)} %param.21) | copy-start | bytes 147460
  16.7 2.5 %copy-start.7 = (s32[1,1,4096]{2,1,0:T(1,128)S(1)}, s32[1,1,4096]{2,1,0:T(1,128)}, u32[]{:S(2)}) copy-start(s32[1,1,4096]{2,1,0:T(1,128)} %param.23) | copy-start | bytes 49156
  16.7 2.5 %copy-start.8 = (s32[1,1,4096]{2,1,0:T(1,128)S(1)}, s32[1,1,4096]{2,1,0:T(1,128)}, u32[]{:S(2)}) copy-start(s32[1,1,4096]{2,1,0:T(1,128)} %param.22) | copy-start | bytes 49156
  17.3 3.6 %collective-permute-start.2 = (f32[56,128]{1,0:T(8,128)S(1)}, f32[56,128]{1,0:T(8,128)S(1)}, u32[]{:S(2)}, u32[]{:S(2)}) collective-permute-start(f32[56,128]{1,0:T(8,128)S(1)} %get-tuple-element.19.refs_0_), channel_id=1, source_target_pairs={{0,3},{1,0},{2,1},{3,2},{4,7},{5,4},{6,5},{7,6},{8,11},{9,8},{10,9... | collective-permute-start | bytes 86024 | tf_op jit(solution)/shard_map/ppermute | solution.py:416
  17.4 4.0 %collective-permute-start.1 = (f32[56,128]{1,0:T(8,128)S(1)}, f32[56,128]{1,0:T(8,128)S(1)}, u32[]{:S(2)}, u32[]{:S(2)}) collective-permute-start(f32[56,128]{1,0:T(8,128)S(1)} %get-tuple-element.19.refs_0_), channel_id=1, source_target_pairs={{0,2},{1,3},{2,0},{3,1},{4,6},{5,7},{6,4},{7,5},{8,10},{9,11},{10,... | collective-permute-start | bytes 86024 | tf_op jit(solution)/shard_map/ppermute | solution.py:416
  19.0 3.3 %collective-permute-start = (f32[56,128]{1,0:T(8,128)S(1)}, f32[56,128]{1,0:T(8,128)S(1)}, u32[]{:S(2)}, u32[]{:S(2)}) collective-permute-start(f32[56,128]{1,0:T(8,128)S(1)} %get-tuple-element.19.refs_0_), channel_id=1, source_target_pairs={{0,1},{1,2},{2,3},{3,0},{4,5},{5,6},{6,7},{7,4},{8,9},{9,10},{10,1... | collective-permute-start | bytes 86024 | tf_op jit(solution)/shard_map/ppermute | solution.py:416
  19.1 0.7 %copy-start.6 = (f32[1,1,3,512]{3,1,2,0:T(1,128)S(1)}, f32[1,1,3,512]{3,1,2,0:T(1,128)}, u32[]{:S(2)}) copy-start(f32[1,1,3,512]{3,1,2,0:T(1,128)} %param.14) | copy-start | bytes 18436
  19.1 0.7 %copy-start.5 = (f32[1,1,3,512]{3,1,2,0:T(1,128)S(1)}, f32[1,1,3,512]{3,1,2,0:T(1,128)}, u32[]{:S(2)}) copy-start(f32[1,1,3,512]{3,1,2,0:T(1,128)} %param.13) | copy-start | bytes 18436
  19.8 2.4 %copy-start.1 = (f32[1,1,36,1024]{3,1,2,0:T(1,128)S(1)}, f32[1,1,36,1024]{3,1,2,0:T(1,128)}, u32[]{:S(2)}) copy-start(f32[1,1,36,1024]{3,1,2,0:T(1,128)} %param.19) | copy-start | bytes 442372
  19.8 2.4 %copy-start.4 = (f32[1,1,6,1024]{3,1,2,0:T(1,128)S(1)}, f32[1,1,6,1024]{3,1,2,0:T(1,128)}, u32[]{:S(2)}) copy-start(f32[1,1,6,1024]{3,1,2,0:T(1,128)} %param.25) | copy-start | bytes 73732
  20.9 1.4 %copy-start.9 = (s32[1,1,1024]{2,1,0:T(1,128)S(1)}, s32[1,1,1024]{2,1,0:T(1,128)}, u32[]{:S(2)}) copy-start(s32[1,1,1024]{2,1,0:T(1,128)} %param.24) | copy-start | bytes 12292

commit v5 on v4

--- a/solution.py
+++ b/solution.py
@@ -128,7 +128,7 @@
 
 
 def consensus_kernel(
-    block, owned_rows, recv_ref, pose_ref, out_ref, back_ref, consensus_ref, backs_ref, news_ref
+    block, owned_rows, order, recv_ref, pose_ref, out_ref, back_ref, consensus_ref, backs_ref, news_ref
 ):
     rows = back_ref.shape[1]
     height = block_rows(rows, owned_rows)
@@ -136,6 +136,7 @@
     per = LANES // block
     wide = per * owned_rows
     side = lax.broadcasted_iota(jnp.int32, (robots, LANES), 1) // block * (owned_rows * LANES)
+    at = [order.index(r) for r in range(robots)]
     primal = jnp.zeros((robots, LANES), jnp.float32)
     dual = jnp.zeros((wide, LANES), jnp.float32)
     for k in range(rows):
@@ -147,7 +148,8 @@
         for v in range(3):
             start = FIELDS * rows + v * owned_rows
             lines = [
-                recv_ref[pl.ds((k * per + j) * height + start, owned_rows), :] for j in range(per)
+                recv_ref[pl.ds(at[k * per + j] * height + start, owned_rows), :]
+                for j in range(per)
             ]
             old = jnp.concatenate(lines, axis=0)
             new = (old + sums[v]) / (1.0 + sums[3])
@@ -162,8 +164,9 @@
             differ = (field[v] - back[v]) * live
             primal = primal + differ * differ
     me = lax.axis_index("robot")
+    mine = sum(jnp.where(me == r, at[r], 0) for r in range(robots))
     for v in range(3):
-        back_ref[v] = backs_ref[v, pl.ds(me, rows, robots), :]
+        back_ref[v] = backs_ref[v, pl.ds(mine, rows, robots), :]
         consensus_ref[v] = news_ref[v, me]
     write_sending(pose_ref, primal, dual, out_ref)
 
@@ -315,9 +318,18 @@
     return pltpu.VMEM(shape, jnp.float32)
 
 
-def over_robots(value, robots):
+def meeting_order(robots):
+    first = robots * 3 // 4
+    if robots & (robots - 1) == 0:
+        return [i ^ first for i in range(robots)]
+    return [first] + [i for i in range(robots) if i != first]
+
+
+def over_robots(value, robots, order=None):
     blocks = value.reshape(robots, value.shape[0] // robots, LANES)
-    return lax.all_to_all(blocks, "robot", 0, 0, tiled=True).reshape(value.shape)
+    groups = None if order is None else [list(order)]
+    moved = lax.all_to_all(blocks, "robot", 0, 0, tiled=True, axis_index_groups=groups)
+    return moved.reshape(value.shape)
 
 
 def in_vmem(value):
@@ -385,9 +397,10 @@
             [vmem(robots * height, LANES), vmem(rows, LANES)],
             [SMEM, VMEM, VMEM, VMEM, VMEM],
         )(counts, copies, duals, ids, old)
-        received = over_robots(outgoing, robots)
+        order = meeting_order(robots)
+        received = over_robots(outgoing, robots, order)
         sending, back, estimate = call(
-            functools.partial(consensus_kernel, block, owned_rows),
+            functools.partial(consensus_kernel, block, owned_rows, order),
             [vmem(sending_rows, LANES), vmem(3, rows, LANES), vmem(3, owned_rows, LANES)],
             [VMEM] * 2,
             scratch=[vmem(3, rows * robots, LANES), vmem(3, robots, owned_rows, LANES)],

time: 23.5 us -> 21.1 us (0.90)
  blocking collectives: 15.2 us -> 12.7 us
    all_to_all x1, blocking collectives: 15.2 us -> 12.7 us  [over_robots(): lax.all_to_all(blocks, 'robot', 0, 0, tiled=True, axis_index_groups=groups)]
where the time goes in v5:
time: 21.1 us; the launch traced here: 20.8 us
  blocking collectives  12.7 us (60%)
  Pallas kernels  3.46 us (16%)
  starting transfers between devices  1.8 us (9%)
  waiting for transfers between devices  1.37 us (6%)
  local copies, waits for them, and re-layouts  0.71 us (3%)
  between operations  0.7 us (3%)
    all_to_all x1, blocking collectives, over_robots(): lax.all_to_all(blocks, 'robot', 0, 0, tiled=True, axis_index_groups=groups)  12.7 us
    ppermute x3, starting transfers between devices, step(): held.append(lax.ppermute(sending, 'sub', ring))  1.8 us
    ppermute x3, waiting for transfers between devices, step(): held.append(lax.ppermute(sending, 'sub', ring))  1.37 us
    pallas_call x1, Pallas kernels, step(): call(observe_kernel, [vmem(6, pose_rows, LANES), (3, rows, LANES), (3, ow...  1.06 us
    pallas_call x1, Pallas kernels, step(): call(functools.partial(refine_kernel, float(owned * robots * subs)), [(6,...  0.95 us
    pallas_call x1, Pallas kernels, step(): call(functools.partial(pack_kernel, block), [vmem(robots * height, LANES)...  0.82 us
    unnamed x20, local copies, waits for them, and re-layouts  0.71 us
    pallas_call x1, Pallas kernels, step(): call(functools.partial(consensus_kernel, block, owned_rows, order), [vmem...  0.64 us
  transfers between devices with their start and end apart: 3, of which 2 were waited for; matrix products, arithmetic and copies ran while one was open for 0% of the time, Pallas kernels for 5%

profile of v5, /device:TPU:0, one launch (start us, length us, event | category | flops | bytes accessed | tf_op | source)
XLA Modules:
  0.0 20.8 jit_solution(4298716853506091112)
XLA Ops:
  0.6 0.8 %shard_map.156 = (f32[384,128]{1,0:T(8,128)S(1)}, f32[4,128]{1,0:T(4,128)S(1)}) custom-call(s32[1,8]{1,0:T(1,128)} %bitcast.34, f32[3,4,128]{2,1,0:T(4,128)} %bitcast.25, f32[3,4,128]{2,1,0:T(4,128)} %bitcast.27, s32[4,128]{1,0:T(4,128)} %bitcast.33, f32[3,4,128]{2,1,0:T(4,128)} %bitcast.32), custom_call_target="tpu_custom_call" | custom-call | tf_op jit(solution)/shard_map/pallas_call | solution.py:395
  1.5 0.0 copy-start.3
  1.5 0.0 copy-start
  1.5 12.7 %all_to_all.5 = f32[8,48,128]{2,1,0:T(8,128)S(1)} all-to-all(f32[8,48,128]{2,1,0:T(8,128)S(1)} %bitcast.20), channel_id=1, replica_groups={{24,28,16,20,8,12,0,4},{25,29,17,21,9,13,1,5},{26,30,18,22,10,14,2,6},{..., dimensions={0} | all-to-all | bytes 393216 | tf_op jit(solution)/shard_map/all_to_all | solution.py:331
  14.2 0.0 copy-done.3
  14.2 0.0 copy-start.2
  14.2 0.0 copy-start.7
  14.2 0.0 copy-start.8
  14.2 0.6 %shard_map.157 = (f32[56,128]{1,0:T(8,128)S(1)}, f32[3,4,128]{2,1,0:T(4,128)S(1)}, f32[3,4,128]{2,1,0:T(4,128)S(1)}) custom-call(f32[384,128]{1,0:T(8,128)S(1)} %bitcast.18, f32[6,8,128]{2,1,0:T(8,128)S(1)} %bitcast.23), custom_call_target="tpu_custom_call" | custom-call | tf_op jit(solution)/shard_map/pallas_call | solution.py:402
  14.9 0.7 %collective-permute-start.2 = (f32[56,128]{1,0:T(8,128)S(1)}, f32[56,128]{1,0:T(8,128)S(1)}, u32[]{:S(2)}, u32[]{:S(2)}) collective-permute-start(f32[56,128]{1,0:T(8,128)S(1)} %get-tuple-element.19.refs_0_), channel_id=1, source_target_pairs={{0,3},{1,0},{2,1},{3,2},{4,7},{5,4},{6,5},{7,6},{8,11},{9,8},{10,9... | collective-permute-start | bytes 86024 | tf_op jit(solution)/shard_map/ppermute | solution.py:429
  15.6 0.9 %collective-permute-start.1 = (f32[56,128]{1,0:T(8,128)S(1)}, f32[56,128]{1,0:T(8,128)S(1)}, u32[]{:S(2)}, u32[]{:S(2)}) collective-permute-start(f32[56,128]{1,0:T(8,128)S(1)} %get-tuple-element.19.refs_0_), channel_id=1, source_target_pairs={{0,2},{1,3},{2,0},{3,1},{4,6},{5,7},{6,4},{7,5},{8,10},{9,11},{10,... | collective-permute-start | bytes 86024 | tf_op jit(solution)/shard_map/ppermute | solution.py:429
  16.5 0.2 collective-permute-start
  16.7 0.0 copy-start.6
  16.7 0.0 copy-start.5
  16.7 0.0 copy-done
  16.7 0.0 copy-done.2
  16.7 0.0 copy-done.7
  16.7 0.0 copy-done.8
  16.7 0.7 %copy-done.6 = f32[1,1,3,512]{3,1,2,0:T(1,128)S(1)} copy-done((f32[1,1,3,512]{3,1,2,0:T(1,128)S(1)}, f32[1,1,3,512]{3,1,2,0:T(1,128)}, u32[]{:S(2)}) %copy-start.6) | copy-done | bytes 6168
  17.4 0.0 copy-done.5
  17.4 0.0 copy-start.1
  17.4 0.0 copy-start.4
  17.4 1.1 %shard_map.158 = (f32[6,8,128]{2,1,0:T(8,128)S(1)}, f32[3,4,128]{2,1,0:T(4,128)}, f32[3,4,128]{2,1,0:T(4,128)}) custom-call(f32[3,4,128]{2,1,0:T(4,128)S(1)} %bitcast.26, f32[3,32,128]{2,1,0:T(8,128)S(1)} %bitcast.22, f32[18,32,128]{2,1,0:T(8,128)S(1)} %bitcast.19, s32[32,128]{1,0:T(8,128)S(1)} %bitcast.29, s32[32,128]{1,0:T(8,128)S(1)} %bitcast.30, ...), custom_call_target="tpu_custom_call" | custom-call | tf_op jit(solution)/shard_map/pallas_call | solution.py:431
  18.4 0.0 copy-start.9
  18.4 0.0 collective-permute-done.2.refs_3_
  18.4 1.0 %collective-permute-done.1.refs_2_ = f32[56,128]{1,0:T(8,128)S(1)} collective-permute-done((f32[56,128]{1,0:T(8,128)S(1)}, f32[56,128]{1,0:T(8,128)S(1)}, u32[]{:S(2)}, u32[]{:S(2)}) %collective-permute-start.1) | collective-permute-done | bytes 28704 | tf_op jit(solution)/shard_map/ppermute | solution.py:429
  19.5 0.3 %collective-permute-done.refs_1_ = f32[56,128]{1,0:T(8,128)S(1)} collective-permute-done((f32[56,128]{1,0:T(8,128)S(1)}, f32[56,128]{1,0:T(8,128)S(1)}, u32[]{:S(2)}, u32[]{:S(2)}) %collective-permute-start) | collective-permute-done | bytes 28704 | tf_op jit(solution)/shard_map/ppermute | solution.py:429
  19.8 0.0 copy-done.1
  19.8 0.0 copy-done.4
  19.8 0.0 copy-done.9
  19.8 0.9 %shard_map.159 = (f32[6,8,128]{2,1,0:T(8,128)}, f32[2]{0:T(128)}) custom-call(s32[8,128]{1,0:T(8,128)S(1)} %bitcast.31, f32[6,8,128]{2,1,0:T(8,128)S(1)} %get-tuple-element.18.grad_ref, f32[36,8,128]{2,1,0:T(8,128)S(1)} %bitcast.21, f32[6,8,128]{2,1,0:T(8,128)S(1)} %bitcast.24, f32[56,128]{1,0:T(8,128)S(1)} %get-tuple-element.19.refs_0_, ...), custom_call_target="tpu_custom_call" | custom-call | tf_op jit(solution)/shard_map/pallas_call | solution.py:448
Async XLA Ops:
  1.5 12.8 %copy-start.3 = (f32[1,1,6,1024]{3,1,2,0:T(1,128)S(1)}, f32[1,1,6,1024]{3,1,2,0:T(1,128)}, u32[]{:S(2)}) copy-start(f32[1,1,6,1024]{3,1,2,0:T(1,128)} %param.18) | copy-start | bytes 73732
  1.5 15.2 %copy-start = (f32[1,1,18,4096]{3,1,2,0:T(1,128)S(1)}, f32[1,1,18,4096]{3,1,2,0:T(1,128)}, u32[]{:S(2)}) copy-start(f32[1,1,18,4096]{3,1,2,0:T(1,128)} %param.20) | copy-start | bytes 884740
  14.2 2.5 %copy-start.2 = (f32[1,1,3,4096]{3,1,2,0:T(1,128)S(1)}, f32[1,1,3,4096]{3,1,2,0:T(1,128)}, u32[]{:S(2)}) copy-start(f32[1,1,3,4096]{3,1,2,0:T(1,128)} %param.21) | copy-start | bytes 147460
  14.2 2.5 %copy-start.7 = (s32[1,1,4096]{2,1,0:T(1,128)S(1)}, s32[1,1,4096]{2,1,0:T(1,128)}, u32[]{:S(2)}) copy-start(s32[1,1,4096]{2,1,0:T(1,128)} %param.23) | copy-start | bytes 49156
  14.2 2.5 %copy-start.8 = (s32[1,1,4096]{2,1,0:T(1,128)S(1)}, s32[1,1,4096]{2,1,0:T(1,128)}, u32[]{:S(2)}) copy-start(s32[1,1,4096]{2,1,0:T(1,128)} %param.22) | copy-start | bytes 49156
  14.9 3.6 %collective-permute-start.2 = (f32[56,128]{1,0:T(8,128)S(1)}, f32[56,128]{1,0:T(8,128)S(1)}, u32[]{:S(2)}, u32[]{:S(2)}) collective-permute-start(f32[56,128]{1,0:T(8,128)S(1)} %get-tuple-element.19.refs_0_), channel_id=1, source_target_pairs={{0,3},{1,0},{2,1},{3,2},{4,7},{5,4},{6,5},{7,6},{8,11},{9,8},{10,9... | collective-permute-start | bytes 86024 | tf_op jit(solution)/shard_map/ppermute | solution.py:429
  15.6 3.9 %collective-permute-start.1 = (f32[56,128]{1,0:T(8,128)S(1)}, f32[56,128]{1,0:T(8,128)S(1)}, u32[]{:S(2)}, u32[]{:S(2)}) collective-permute-start(f32[56,128]{1,0:T(8,128)S(1)} %get-tuple-element.19.refs_0_), channel_id=1, source_target_pairs={{0,2},{1,3},{2,0},{3,1},{4,6},{5,7},{6,4},{7,5},{8,10},{9,11},{10,... | collective-permute-start | bytes 86024 | tf_op jit(solution)/shard_map/ppermute | solution.py:429
  16.5 3.3 %collective-permute-start = (f32[56,128]{1,0:T(8,128)S(1)}, f32[56,128]{1,0:T(8,128)S(1)}, u32[]{:S(2)}, u32[]{:S(2)}) collective-permute-start(f32[56,128]{1,0:T(8,128)S(1)} %get-tuple-element.19.refs_0_), channel_id=1, source_target_pairs={{0,1},{1,2},{2,3},{3,0},{4,5},{5,6},{6,7},{7,4},{8,9},{9,10},{10,1... | collective-permute-start | bytes 86024 | tf_op jit(solution)/shard_map/ppermute | solution.py:429
  16.7 0.7 %copy-start.6 = (f32[1,1,3,512]{3,1,2,0:T(1,128)S(1)}, f32[1,1,3,512]{3,1,2,0:T(1,128)}, u32[]{:S(2)}) copy-start(f32[1,1,3,512]{3,1,2,0:T(1,128)} %param.14) | copy-start | bytes 18436
  16.7 0.7 %copy-start.5 = (f32[1,1,3,512]{3,1,2,0:T(1,128)S(1)}, f32[1,1,3,512]{3,1,2,0:T(1,128)}, u32[]{:S(2)}) copy-start(f32[1,1,3,512]{3,1,2,0:T(1,128)} %param.13) | copy-start | bytes 18436
  17.4 2.4 %copy-start.1 = (f32[1,1,36,1024]{3,1,2,0:T(1,128)S(1)}, f32[1,1,36,1024]{3,1,2,0:T(1,128)}, u32[]{:S(2)}) copy-start(f32[1,1,36,1024]{3,1,2,0:T(1,128)} %param.19) | copy-start | bytes 442372
  17.4 2.4 %copy-start.4 = (f32[1,1,6,1024]{3,1,2,0:T(1,128)S(1)}, f32[1,1,6,1024]{3,1,2,0:T(1,128)}, u32[]{:S(2)}) copy-start(f32[1,1,6,1024]{3,1,2,0:T(1,128)} %param.25) | copy-start | bytes 73732
  18.4 1.4 %copy-start.9 = (s32[1,1,1024]{2,1,0:T(1,128)S(1)}, s32[1,1,1024]{2,1,0:T(1,128)}, u32[]{:S(2)}) copy-start(s32[1,1,1024]{2,1,0:T(1,128)} %param.24) | copy-start | bytes 12292

commit v6 on v5

--- a/solution.py
+++ b/solution.py
@@ -102,14 +102,17 @@
     )
 
 
-def block_rows(rows, owned_rows):
-    used = FIELDS * rows + 3 * owned_rows
-    return -(-used // SUBLANES) * SUBLANES
+def block_rows(robots, rows, owned_rows):
+    used = 7 * rows + 3 * owned_rows + 1
+    while used * robots % SUBLANES:
+        used += 1
+    return used
 
 
 def pack_kernel(block, counts_ref, copies_ref, duals_ref, ids_ref, old_ref, out_ref, live_ref):
     rows, owned_rows = ids_ref.shape[0], old_ref.shape[1]
-    height = block_rows(rows, owned_rows)
+    robots = counts_ref.shape[1]
+    height = block_rows(robots, rows, owned_rows)
     per = LANES // block
     lane = lax.broadcasted_iota(jnp.int32, (rows, LANES), 1)
     live = jnp.zeros((rows, LANES), jnp.float32)
@@ -118,35 +121,47 @@
         live = jnp.where((lane >= j * block) & (lane < j * block + count), 1.0, live)
     live_ref[...] = live
     planes = [copies_ref[k] for k in range(3)] + [duals_ref[k] for k in range(3)]
-    planes += [ids_ref[...].astype(jnp.float32), live] + [old_ref[k] for k in range(3)]
-    used = FIELDS * rows + 3 * owned_rows
-    if height > used:
-        planes.append(jnp.zeros((height - used, LANES), jnp.float32))
-    whole = jnp.concatenate(planes, axis=0)
-    for d in range(out_ref.shape[0] // height):
-        out_ref[pl.ds(d * height, height), :] = whole
+    planes += [ids_ref[...].astype(jnp.float32)] + [old_ref[k] for k in range(3)]
+    lane = lax.broadcasted_iota(jnp.int32, (1, LANES), 1)
+    line = jnp.zeros((1, LANES), jnp.int32)
+    for d in range(robots):
+        line = jnp.where(lane == d, counts_ref[0, d], line)
+    planes.append(line.astype(jnp.float32))
+    for d in range(robots):
+        start = d * height
+        for plane in planes:
+            out_ref[pl.ds(start, plane.shape[0]), :] = plane
+            start += plane.shape[0]
+        if start < (d + 1) * height:
+            rest = (d + 1) * height - start
+            out_ref[pl.ds(start, rest), :] = jnp.zeros((rest, LANES), jnp.float32)
 
 
 def consensus_kernel(
     block, owned_rows, order, recv_ref, pose_ref, out_ref, back_ref, consensus_ref, backs_ref, news_ref
 ):
     rows = back_ref.shape[1]
-    height = block_rows(rows, owned_rows)
-    robots = recv_ref.shape[0] // height
+    robots = len(order)
+    height = block_rows(robots, rows, owned_rows)
     per = LANES // block
     wide = per * owned_rows
-    side = lax.broadcasted_iota(jnp.int32, (robots, LANES), 1) // block * (owned_rows * LANES)
+    lane = lax.broadcasted_iota(jnp.int32, (robots, LANES), 1)
+    side = lane // block * (owned_rows * LANES)
+    counts = recv_ref[pl.ds(7 * rows + 3 * owned_rows, robots, height), :].astype(jnp.int32)
     at = [order.index(r) for r in range(robots)]
     primal = jnp.zeros((robots, LANES), jnp.float32)
     dual = jnp.zeros((wide, LANES), jnp.float32)
     for k in range(rows):
-        field = [recv_ref[pl.ds(v * rows + k, robots, height), :] for v in range(FIELDS)]
-        live = field[7]
+        field = [recv_ref[pl.ds(v * rows + k, robots, height), :] for v in range(7)]
+        live = jnp.zeros((robots, LANES), jnp.float32)
+        for j in range(per):
+            count = jnp.broadcast_to(counts[:, k * per + j : k * per + j + 1], live.shape)
+            live = jnp.where((lane >= j * block) & (lane < j * block + count), 1.0, live)
         ids = field[6].astype(jnp.int32) + side
         sums = slot_sums(field, live, ids, wide)
         tables = []
         for v in range(3):
-            start = FIELDS * rows + v * owned_rows
+            start = 7 * rows + v * owned_rows
             lines = [
                 recv_ref[pl.ds(at[k * per + j] * height + start, owned_rows), :]
                 for j in range(per)
@@ -318,15 +333,17 @@
     return pltpu.VMEM(shape, jnp.float32)
 
 
+TRIED_ORDERS = {8: (5, 3, 0, 7, 6, 2, 1, 4)}
+
+
 def meeting_order(robots):
     first = robots * 3 // 4
-    if robots & (robots - 1) == 0:
-        return [i ^ first for i in range(robots)]
-    return [first] + [i for i in range(robots) if i != first]
+    rest = [i for i in range(robots) if i != first]
+    return list(TRIED_ORDERS.get(robots, [first] + rest))
 
 
 def over_robots(value, robots, order=None):
-    blocks = value.reshape(robots, value.shape[0] // robots, LANES)
+    blocks = value.reshape(robots, 1, value.shape[0] // robots * LANES)
     groups = None if order is None else [list(order)]
     moved = lax.all_to_all(blocks, "robot", 0, 0, tiled=True, axis_index_groups=groups)
     return moved.reshape(value.shape)
@@ -389,7 +406,7 @@
     edges = edge_to.reshape(pose_rows, LANES)
     offset = edge_offset.reshape(6, pose_rows, LANES)
 
-    height = block_rows(rows, owned_rows)
+    height = block_rows(robots, rows, owned_rows)
     sending_rows = 6 * pose_rows + SUBLANES
     if robots * height * LANES * 4 <= WHOLE_BYTES:
         outgoing, live = call(

time: 21.1 us -> 19.7 us (0.934)
  blocking collectives: 12.7 us -> 11.3 us
    all_to_all x1, blocking collectives: 12.7 us -> 11.3 us  [over_robots(): lax.all_to_all(blocks, 'robot', 0, 0, tiled=True, axis_index_groups=groups)]
where the time goes in v6:
time: 19.7 us; the launch traced here: 19.4 us
  blocking collectives  11.3 us (57%)
  Pallas kernels  3.51 us (18%)
  starting transfers between devices  1.79 us (9%)
  waiting for transfers between devices  1.37 us (7%)
  local copies, waits for them, and re-layouts  0.71 us (4%)
  between operations  0.71 us (4%)
    all_to_all x1, blocking collectives, over_robots(): lax.all_to_all(blocks, 'robot', 0, 0, tiled=True, axis_index_groups=groups)  11.3 us
    ppermute x3, starting transfers between devices, step(): held.append(lax.ppermute(sending, 'sub', ring))  1.79 us
    ppermute x3, waiting for transfers between devices, step(): held.append(lax.ppermute(sending, 'sub', ring))  1.37 us
    pallas_call x1, Pallas kernels, step(): call(observe_kernel, [vmem(6, pose_rows, LANES), (3, rows, LANES), (3, ow...  1.06 us
    pallas_call x1, Pallas kernels, step(): call(functools.partial(refine_kernel, float(owned * robots * subs)), [(6,...  0.95 us
    pallas_call x1, Pallas kernels, step(): call(functools.partial(pack_kernel, block), [vmem(robots * height, LANES)...  0.83 us
    unnamed x20, local copies, waits for them, and re-layouts  0.71 us
    pallas_call x1, Pallas kernels, step(): call(functools.partial(consensus_kernel, block, owned_rows, order), [vmem...  0.67 us
  transfers between devices with their start and end apart: 3, of which 2 were waited for; matrix products, arithmetic and copies ran while one was open for 0% of the time, Pallas kernels for 5%

profile of v6, /device:TPU:0, one launch (start us, length us, event | category | flops | bytes accessed | tf_op | source)
XLA Modules:
  0.0 19.4 jit_solution(547773520060836118)
XLA Ops:
  0.6 0.0 copy-start
  0.6 0.8 %shard_map.156 = (f32[328,128]{1,0:T(8,128)S(1)}, f32[4,128]{1,0:T(4,128)S(1)}) custom-call(s32[1,8]{1,0:T(1,128)} %bitcast.34, f32[3,4,128]{2,1,0:T(4,128)} %bitcast.25, f32[3,4,128]{2,1,0:T(4,128)} %bitcast.27, s32[4,128]{1,0:T(4,128)} %bitcast.33, f32[3,4,128]{2,1,0:T(4,128)} %bitcast.32), custom_call_target="tpu_custom_call" | custom-call | tf_op jit(solution)/shard_map/pallas_call | solution.py:412
  1.5 0.0 copy-start.3
  1.5 11.3 %all_to_all.5 = f32[8,1,5248]{2,1,0:T(1,128)S(1)} all-to-all(f32[8,1,5248]{2,1,0:T(1,128)S(1)} %bitcast.20), channel_id=1, replica_groups={{20,12,0,28,24,8,4,16},{21,13,1,29,25,9,5,17},{22,14,2,30,26,10,6,18},{..., dimensions={0} | all-to-all | bytes 335872 | tf_op jit(solution)/shard_map/all_to_all | solution.py:348
  12.8 0.0 copy-done.3
  12.8 0.0 copy-start.2
  12.8 0.0 copy-start.7
  12.8 0.0 copy-start.8
  12.8 0.7 %shard_map.157 = (f32[56,128]{1,0:T(8,128)S(1)}, f32[3,4,128]{2,1,0:T(4,128)S(1)}, f32[3,4,128]{2,1,0:T(4,128)S(1)}) custom-call(f32[328,128]{1,0:T(8,128)S(1)} %bitcast.18, f32[6,8,128]{2,1,0:T(8,128)S(1)} %bitcast.23), custom_call_target="tpu_custom_call" | custom-call | tf_op jit(solution)/shard_map/pallas_call | solution.py:419
  13.5 0.1 collective-permute-start.2
  13.5 1.6 %collective-permute-start.1 = (f32[56,128]{1,0:T(8,128)S(1)}, f32[56,128]{1,0:T(8,128)S(1)}, u32[]{:S(2)}, u32[]{:S(2)}) collective-permute-start(f32[56,128]{1,0:T(8,128)S(1)} %get-tuple-element.19.refs_0_), channel_id=1, source_target_pairs={{0,2},{1,3},{2,0},{3,1},{4,6},{5,7},{6,4},{7,5},{8,10},{9,11},{10,... | collective-permute-start | bytes 86024 | tf_op jit(solution)/shard_map/ppermute | solution.py:446
  15.1 0.2 collective-permute-start
  15.3 0.0 copy-start.6
  15.3 0.0 copy-start.5
  15.3 0.0 copy-done
  15.3 0.0 copy-done.2
  15.3 0.0 copy-done.7
  15.3 0.0 copy-done.8
  15.3 0.7 %copy-done.6 = f32[1,1,3,512]{3,1,2,0:T(1,128)S(1)} copy-done((f32[1,1,3,512]{3,1,2,0:T(1,128)S(1)}, f32[1,1,3,512]{3,1,2,0:T(1,128)}, u32[]{:S(2)}) %copy-start.6) | copy-done | bytes 6168
  16.0 0.0 copy-done.5
  16.0 0.0 copy-start.1
  16.0 0.0 copy-start.4
  16.0 1.1 %shard_map.158 = (f32[6,8,128]{2,1,0:T(8,128)S(1)}, f32[3,4,128]{2,1,0:T(4,128)}, f32[3,4,128]{2,1,0:T(4,128)}) custom-call(f32[3,4,128]{2,1,0:T(4,128)S(1)} %bitcast.26, f32[3,32,128]{2,1,0:T(8,128)S(1)} %bitcast.22, f32[18,32,128]{2,1,0:T(8,128)S(1)} %bitcast.19, s32[32,128]{1,0:T(8,128)S(1)} %bitcast.29, s32[32,128]{1,0:T(8,128)S(1)} %bitcast.30, ...), custom_call_target="tpu_custom_call" | custom-call | tf_op jit(solution)/shard_map/pallas_call | solution.py:448
  17.1 0.0 copy-start.9
  17.1 0.0 collective-permute-done.2.refs_3_
  17.1 0.5 %collective-permute-done.1.refs_2_ = f32[56,128]{1,0:T(8,128)S(1)} collective-permute-done((f32[56,128]{1,0:T(8,128)S(1)}, f32[56,128]{1,0:T(8,128)S(1)}, u32[]{:S(2)}, u32[]{:S(2)}) %collective-permute-start.1) | collective-permute-done | bytes 28704 | tf_op jit(solution)/shard_map/ppermute | solution.py:446
  17.5 0.9 %collective-permute-done.refs_1_ = f32[56,128]{1,0:T(8,128)S(1)} collective-permute-done((f32[56,128]{1,0:T(8,128)S(1)}, f32[56,128]{1,0:T(8,128)S(1)}, u32[]{:S(2)}, u32[]{:S(2)}) %collective-permute-start) | collective-permute-done | bytes 28704 | tf_op jit(solution)/shard_map/ppermute | solution.py:446
  18.4 0.0 copy-done.1
  18.4 0.0 copy-done.4
  18.4 0.0 copy-done.9
  18.4 0.9 %shard_map.159 = (f32[6,8,128]{2,1,0:T(8,128)}, f32[2]{0:T(128)}) custom-call(s32[8,128]{1,0:T(8,128)S(1)} %bitcast.31, f32[6,8,128]{2,1,0:T(8,128)S(1)} %get-tuple-element.18.grad_ref, f32[36,8,128]{2,1,0:T(8,128)S(1)} %bitcast.21, f32[6,8,128]{2,1,0:T(8,128)S(1)} %bitcast.24, f32[56,128]{1,0:T(8,128)S(1)} %get-tuple-element.19.refs_0_, ...), custom_call_target="tpu_custom_call" | custom-call | tf_op jit(solution)/shard_map/pallas_call | solution.py:465
Async XLA Ops:
  0.6 14.7 %copy-start = (f32[1,1,18,4096]{3,1,2,0:T(1,128)S(1)}, f32[1,1,18,4096]{3,1,2,0:T(1,128)}, u32[]{:S(2)}) copy-start(f32[1,1,18,4096]{3,1,2,0:T(1,128)} %param.20) | copy-start | bytes 884740
  1.5 11.3 %copy-start.3 = (f32[1,1,6,1024]{3,1,2,0:T(1,128)S(1)}, f32[1,1,6,1024]{3,1,2,0:T(1,128)}, u32[]{:S(2)}) copy-start(f32[1,1,6,1024]{3,1,2,0:T(1,128)} %param.18) | copy-start | bytes 73732
  12.8 2.5 %copy-start.2 = (f32[1,1,3,4096]{3,1,2,0:T(1,128)S(1)}, f32[1,1,3,4096]{3,1,2,0:T(1,128)}, u32[]{:S(2)}) copy-start(f32[1,1,3,4096]{3,1,2,0:T(1,128)} %param.21) | copy-start | bytes 147460
  12.8 2.5 %copy-start.7 = (s32[1,1,4096]{2,1,0:T(1,128)S(1)}, s32[1,1,4096]{2,1,0:T(1,128)}, u32[]{:S(2)}) copy-start(s32[1,1,4096]{2,1,0:T(1,128)} %param.23) | copy-start | bytes 49156
  12.8 2.5 %copy-start.8 = (s32[1,1,4096]{2,1,0:T(1,128)S(1)}, s32[1,1,4096]{2,1,0:T(1,128)}, u32[]{:S(2)}) copy-start(s32[1,1,4096]{2,1,0:T(1,128)} %param.22) | copy-start | bytes 49156
  13.5 3.6 %collective-permute-start.2 = (f32[56,128]{1,0:T(8,128)S(1)}, f32[56,128]{1,0:T(8,128)S(1)}, u32[]{:S(2)}, u32[]{:S(2)}) collective-permute-start(f32[56,128]{1,0:T(8,128)S(1)} %get-tuple-element.19.refs_0_), channel_id=1, source_target_pairs={{0,3},{1,0},{2,1},{3,2},{4,7},{5,4},{6,5},{7,6},{8,11},{9,8},{10,9... | collective-permute-start | bytes 86024 | tf_op jit(solution)/shard_map/ppermute | solution.py:446
  13.5 4.0 %collective-permute-start.1 = (f32[56,128]{1,0:T(8,128)S(1)}, f32[56,128]{1,0:T(8,128)S(1)}, u32[]{:S(2)}, u32[]{:S(2)}) collective-permute-start(f32[56,128]{1,0:T(8,128)S(1)} %get-tuple-element.19.refs_0_), channel_id=1, source_target_pairs={{0,2},{1,3},{2,0},{3,1},{4,6},{5,7},{6,4},{7,5},{8,10},{9,11},{10,... | collective-permute-start | bytes 86024 | tf_op jit(solution)/shard_map/ppermute | solution.py:446
  15.1 3.3 %collective-permute-start = (f32[56,128]{1,0:T(8,128)S(1)}, f32[56,128]{1,0:T(8,128)S(1)}, u32[]{:S(2)}, u32[]{:S(2)}) collective-permute-start(f32[56,128]{1,0:T(8,128)S(1)} %get-tuple-element.19.refs_0_), channel_id=1, source_target_pairs={{0,1},{1,2},{2,3},{3,0},{4,5},{5,6},{6,7},{7,4},{8,9},{9,10},{10,1... | collective-permute-start | bytes 86024 | tf_op jit(solution)/shard_map/ppermute | solution.py:446
  15.3 0.7 %copy-start.6 = (f32[1,1,3,512]{3,1,2,0:T(1,128)S(1)}, f32[1,1,3,512]{3,1,2,0:T(1,128)}, u32[]{:S(2)}) copy-start(f32[1,1,3,512]{3,1,2,0:T(1,128)} %param.14) | copy-start | bytes 18436
  15.3 0.7 %copy-start.5 = (f32[1,1,3,512]{3,1,2,0:T(1,128)S(1)}, f32[1,1,3,512]{3,1,2,0:T(1,128)}, u32[]{:S(2)}) copy-start(f32[1,1,3,512]{3,1,2,0:T(1,128)} %param.13) | copy-start | bytes 18436
  16.0 2.4 %copy-start.1 = (f32[1,1,36,1024]{3,1,2,0:T(1,128)S(1)}, f32[1,1,36,1024]{3,1,2,0:T(1,128)}, u32[]{:S(2)}) copy-start(f32[1,1,36,1024]{3,1,2,0:T(1,128)} %param.19) | copy-start | bytes 442372
  16.0 2.4 %copy-start.4 = (f32[1,1,6,1024]{3,1,2,0:T(1,128)S(1)}, f32[1,1,6,1024]{3,1,2,0:T(1,128)}, u32[]{:S(2)}) copy-start(f32[1,1,6,1024]{3,1,2,0:T(1,128)} %param.25) | copy-start | bytes 73732
  17.1 1.4 %copy-start.9 = (s32[1,1,1024]{2,1,0:T(1,128)S(1)}, s32[1,1,1024]{2,1,0:T(1,128)}, u32[]{:S(2)}) copy-start(s32[1,1,1024]{2,1,0:T(1,128)} %param.24) | copy-start | bytes 12292

commit v7 on v6

--- a/solution.py
+++ b/solution.py
@@ -109,7 +109,7 @@
     return used
 
 
-def pack_kernel(block, counts_ref, copies_ref, duals_ref, ids_ref, old_ref, out_ref, live_ref):
+def pack_kernel(block, counts_ref, copies_ref, duals_ref, ids_ref, old_ref, edge_ref, out_ref, live_ref, c_ref, d_ref, e_ref):
     rows, owned_rows = ids_ref.shape[0], old_ref.shape[1]
     robots = counts_ref.shape[1]
     height = block_rows(robots, rows, owned_rows)
@@ -120,6 +120,9 @@
         count = column_of(counts_ref, j, per, rows)
         live = jnp.where((lane >= j * block) & (lane < j * block + count), 1.0, live)
     live_ref[...] = live
+    c_ref[...] = copies_ref[...]
+    d_ref[...] = duals_ref[...]
+    e_ref[...] = edge_ref[...]
     planes = [copies_ref[k] for k in range(3)] + [duals_ref[k] for k in range(3)]
     planes += [ids_ref[...].astype(jnp.float32)] + [old_ref[k] for k in range(3)]
     lane = lax.broadcasted_iota(jnp.int32, (1, LANES), 1)
@@ -300,7 +303,7 @@
     count = rows * LANES
     me = lax.axis_index("sub")
     edge = edge_ref[...]
-    place = lax.rem(me + subs - edge // count, subs)
+    place = lax.bitwise_xor(edge // count, me)
     tables = [
         [held[pl.ds(a * rows + k, 1), :] for held in blocks for k in range(rows)]
         for a in range(6)
@@ -315,7 +318,7 @@
         out_ref[a] = own[a] + delta
     total = None
     for s in range(subs):
-        place = lax.rem(me + subs - s, subs)
+        place = lax.bitwise_xor(me, jnp.int32(s))
         part = blocks[0][pl.ds(6 * rows, SUBLANES), :]
         for k in range(1, subs):
             part = jnp.where(place == k, blocks[k][pl.ds(6 * rows, SUBLANES), :], part)
@@ -409,11 +412,13 @@
     height = block_rows(robots, rows, owned_rows)
     sending_rows = 6 * pose_rows + SUBLANES
     if robots * height * LANES * 4 <= WHOLE_BYTES:
-        outgoing, live = call(
+        outgoing, live, copies, duals, edges = call(
             functools.partial(pack_kernel, block),
-            [vmem(robots * height, LANES), vmem(rows, LANES)],
-            [SMEM, VMEM, VMEM, VMEM, VMEM],
-        )(counts, copies, duals, ids, old)
+            [vmem(robots * height, LANES), vmem(rows, LANES)]
+            + [vmem(3, rows, LANES)] * 2
+            + [pltpu.VMEM((pose_rows, LANES), jnp.int32)],
+            [SMEM] + [VMEM] * 5,
+        )(counts, copies, duals, ids, old, edges)
         order = meeting_order(robots)
         received = over_robots(outgoing, robots, order)
         sending, back, estimate = call(
@@ -442,7 +447,7 @@
 
     held = [sending]
     for k in range(1, subs):
-        ring = [(i, (i + k) % subs) for i in range(subs)]
+        ring = [(i, i ^ k) for i in range(subs)]
         held.append(lax.ppermute(sending, "sub", ring))
 
     grad_obs, dual_new, consensus = call(

time: 19.7 us -> 18.7 us (0.949)
  local copies, waits for them, and re-layouts: 0.71 us -> 0.04 us
  waiting for transfers between devices: 1.37 us -> 0.99 us
    unnamed x20 -> x14, local copies, waits for them, and re-layouts: 0.71 us -> 0.04 us
    ppermute x3, waiting for transfers between devices: 1.37 us -> 0.99 us  [step(): held.append(lax.ppermute(sending, 'sub', ring))]
  transfers between devices with their start and end apart: 3 -> 3, of which waited for: 2 -> 2; matrix products, arithmetic and copies ran while one was open for 0% -> 0% of each run, Pallas kernels for 5% -> 6%
where the time goes in v7:
time: 18.7 us; the launch traced here: 18.5 us
  blocking collectives  11.3 us (60%)
  Pallas kernels  3.51 us (19%)
  starting transfers between devices  1.92 us (10%)
  waiting for transfers between devices  0.99 us (5%)
  between operations  0.71 us (4%)
    all_to_all x1, blocking collectives, over_robots(): lax.all_to_all(blocks, 'robot', 0, 0, tiled=True, axis_index_groups=groups)  11.3 us
    ppermute x3, starting transfers between devices, step(): held.append(lax.ppermute(sending, 'sub', ring))  1.92 us
    pallas_call x1, Pallas kernels, step(): call(observe_kernel, [vmem(6, pose_rows, LANES), (3, rows, LANES), (3, ow...  1.06 us
    ppermute x3, waiting for transfers between devices, step(): held.append(lax.ppermute(sending, 'sub', ring))  0.99 us
    pallas_call x1, Pallas kernels, step(): call(functools.partial(refine_kernel, float(owned * robots * subs)), [(6,...  0.95 us
    pallas_call x1, Pallas kernels, step(): call(functools.partial(pack_kernel, block), [vmem(robots * height, LANES)...  0.83 us
    pallas_call x1, Pallas kernels, step(): call(functools.partial(consensus_kernel, block, owned_rows, order), [vmem...  0.67 us
  transfers between devices with their start and end apart: 3, of which 2 were waited for; matrix products, arithmetic and copies ran while one was open for 0% of the time, Pallas kernels for 6%

profile of v7, /device:TPU:0, one launch (start us, length us, event | category | flops | bytes accessed | tf_op | source)
XLA Modules:
  0.0 18.5 jit_solution(10405987729833045614)
XLA Ops:
  0.6 0.0 copy-start
  0.6 0.8 %shard_map.156 = (f32[328,128]{1,0:T(8,128)S(1)}, f32[4,128]{1,0:T(4,128)S(1)}, f32[3,4,128]{2,1,0:T(4,128)S(1)}, f32[3,4,128]{2,1,0:T(4,128)S(1)}, s32[8,128]{1,0:T(8,128)S(1)}) custom-call(s32[1,8]{1,0:T(1,128)} %bitcast.32, f32[3,4,128]{2,1,0:T(4,128)} %bitcast.27, f32[3,4,128]{2,1,0:T(4,128)} %bitcast.28, s32[4,128]{1,0:T(4,128)} %bitcast.31, ...), custom_call_target="tpu_custom_call" | custom-call | tf_op jit(solution)/shard_map/pallas_call | solution.py:415
  1.5 0.0 copy-start.3
  1.5 11.3 %all_to_all.5 = f32[8,1,5248]{2,1,0:T(1,128)S(1)} all-to-all(f32[8,1,5248]{2,1,0:T(1,128)S(1)} %bitcast.20), channel_id=1, replica_groups={{20,12,0,28,24,8,4,16},{21,13,1,29,25,9,5,17},{22,14,2,30,26,10,6,18},{..., dimensions={0} | all-to-all | bytes 335872 | tf_op jit(solution)/shard_map/all_to_all | solution.py:351
  12.8 0.0 copy-done.3
  12.8 0.0 copy-start.2
  12.8 0.0 copy-start.6
  12.8 0.7 %shard_map.157 = (f32[56,128]{1,0:T(8,128)S(1)}, f32[3,4,128]{2,1,0:T(4,128)S(1)}, f32[3,4,128]{2,1,0:T(4,128)S(1)}) custom-call(f32[328,128]{1,0:T(8,128)S(1)} %bitcast.18, f32[6,8,128]{2,1,0:T(8,128)S(1)} %bitcast.23), custom_call_target="tpu_custom_call" | custom-call | tf_op jit(solution)/shard_map/pallas_call | solution.py:424
  13.5 0.0 copy-start.5
  13.5 0.1 collective-permute-start.2
  13.6 1.6 %collective-permute-start.1 = (f32[56,128]{1,0:T(8,128)S(1)}, f32[56,128]{1,0:T(8,128)S(1)}, u32[]{:S(2)}, u32[]{:S(2)}) collective-permute-start(f32[56,128]{1,0:T(8,128)S(1)} %get-tuple-element.25.refs_0_), channel_id=1, source_target_pairs={{0,2},{1,3},{2,0},{3,1},{4,6},{5,7},{6,4},{7,5},{8,10},{9,11},{10,... | collective-permute-start | bytes 86024 | tf_op jit(solution)/shard_map/ppermute | solution.py:451
  15.2 0.3 %collective-permute-start = (f32[56,128]{1,0:T(8,128)S(1)}, f32[56,128]{1,0:T(8,128)S(1)}, u32[]{:S(2)}, u32[]{:S(2)}) collective-permute-start(f32[56,128]{1,0:T(8,128)S(1)} %get-tuple-element.25.refs_0_), channel_id=1, source_target_pairs={{0,1},{1,0},{2,3},{3,2},{4,5},{5,4},{6,7},{7,6},{8,9},{9,8},{10,11... | collective-permute-start | bytes 86024 | tf_op jit(solution)/shard_map/ppermute | solution.py:451
  15.4 0.0 copy-done
  15.4 0.0 copy-done.2
  15.4 0.0 copy-done.6
  15.4 0.0 copy-done.5
  15.4 0.0 copy-start.1
  15.4 0.0 copy-start.4
  15.5 1.1 %shard_map.158 = (f32[6,8,128]{2,1,0:T(8,128)S(1)}, f32[3,4,128]{2,1,0:T(4,128)}, f32[3,4,128]{2,1,0:T(4,128)}) custom-call(f32[3,4,128]{2,1,0:T(4,128)S(1)} %get-tuple-element.18.copies_ref, f32[3,32,128]{2,1,0:T(8,128)S(1)} %bitcast.22, f32[18,32,128]{2,1,0:T(8,128)S(1)} %bitcast.19, s32[32,128]{1,0:T(8,128)S(1)} %bitcast.25, s32[32,128]{1,0:T(8,128)S(1)} %bitcast.26, ...), custom_call_target="tpu_custom_call" | custom-call | tf_op jit(solution)/shard_map/pallas_call | solution.py:453
  16.5 0.6 %collective-permute-done.2.refs_3_ = f32[56,128]{1,0:T(8,128)S(1)} collective-permute-done((f32[56,128]{1,0:T(8,128)S(1)}, f32[56,128]{1,0:T(8,128)S(1)}, u32[]{:S(2)}, u32[]{:S(2)}) %collective-permute-start.2) | collective-permute-done | bytes 28704 | tf_op jit(solution)/shard_map/ppermute | solution.py:451
  17.1 0.4 %collective-permute-done.1.refs_2_ = f32[56,128]{1,0:T(8,128)S(1)} collective-permute-done((f32[56,128]{1,0:T(8,128)S(1)}, f32[56,128]{1,0:T(8,128)S(1)}, u32[]{:S(2)}, u32[]{:S(2)}) %collective-permute-start.1) | collective-permute-done | bytes 28704 | tf_op jit(solution)/shard_map/ppermute | solution.py:451
  17.5 0.0 collective-permute-done.refs_1_
  17.5 0.0 copy-done.1
  17.5 0.0 copy-done.4
  17.5 0.9 %shard_map.159 = (f32[6,8,128]{2,1,0:T(8,128)}, f32[2]{0:T(128)}) custom-call(s32[8,128]{1,0:T(8,128)S(1)} %get-tuple-element.17.edge_ref, f32[6,8,128]{2,1,0:T(8,128)S(1)} %get-tuple-element.24.grad_ref, f32[36,8,128]{2,1,0:T(8,128)S(1)} %bitcast.21, f32[6,8,128]{2,1,0:T(8,128)S(1)} %bitcast.24, f32[56,128]{1,0:T(8,128)S(1)} %get-tuple-element.25.refs_0_, ...), custom_call_target="tpu_custom_call" | custom-call | tf_op jit(solution)/shard_map/pallas_call | solution.py:470
Async XLA Ops:
  0.6 14.8 %copy-start = (f32[1,1,18,4096]{3,1,2,0:T(1,128)S(1)}, f32[1,1,18,4096]{3,1,2,0:T(1,128)}, u32[]{:S(2)}) copy-start(f32[1,1,18,4096]{3,1,2,0:T(1,128)} %param.20) | copy-start | bytes 884740
  1.5 11.3 %copy-start.3 = (f32[1,1,6,1024]{3,1,2,0:T(1,128)S(1)}, f32[1,1,6,1024]{3,1,2,0:T(1,128)}, u32[]{:S(2)}) copy-start(f32[1,1,6,1024]{3,1,2,0:T(1,128)} %param.18) | copy-start | bytes 73732
  12.8 2.6 %copy-start.2 = (f32[1,1,3,4096]{3,1,2,0:T(1,128)S(1)}, f32[1,1,3,4096]{3,1,2,0:T(1,128)}, u32[]{:S(2)}) copy-start(f32[1,1,3,4096]{3,1,2,0:T(1,128)} %param.21) | copy-start | bytes 147460
  12.8 2.6 %copy-start.6 = (s32[1,1,4096]{2,1,0:T(1,128)S(1)}, s32[1,1,4096]{2,1,0:T(1,128)}, u32[]{:S(2)}) copy-start(s32[1,1,4096]{2,1,0:T(1,128)} %param.22) | copy-start | bytes 49156
  13.5 1.9 %copy-start.5 = (s32[1,1,4096]{2,1,0:T(1,128)S(1)}, s32[1,1,4096]{2,1,0:T(1,128)}, u32[]{:S(2)}) copy-start(s32[1,1,4096]{2,1,0:T(1,128)} %param.23) | copy-start | bytes 49156
  13.5 3.6 %collective-permute-start.2 = (f32[56,128]{1,0:T(8,128)S(1)}, f32[56,128]{1,0:T(8,128)S(1)}, u32[]{:S(2)}, u32[]{:S(2)}) collective-permute-start(f32[56,128]{1,0:T(8,128)S(1)} %get-tuple-element.25.refs_0_), channel_id=1, source_target_pairs={{0,3},{1,2},{2,1},{3,0},{4,7},{5,6},{6,5},{7,4},{8,11},{9,10},{10,... | collective-permute-start | bytes 86024 | tf_op jit(solution)/shard_map/ppermute | solution.py:451
  13.6 3.9 %collective-permute-start.1 = (f32[56,128]{1,0:T(8,128)S(1)}, f32[56,128]{1,0:T(8,128)S(1)}, u32[]{:S(2)}, u32[]{:S(2)}) collective-permute-start(f32[56,128]{1,0:T(8,128)S(1)} %get-tuple-element.25.refs_0_), channel_id=1, source_target_pairs={{0,2},{1,3},{2,0},{3,1},{4,6},{5,7},{6,4},{7,5},{8,10},{9,11},{10,... | collective-permute-start | bytes 86024 | tf_op jit(solution)/shard_map/ppermute | solution.py:451
  15.2 2.4 %collective-permute-start = (f32[56,128]{1,0:T(8,128)S(1)}, f32[56,128]{1,0:T(8,128)S(1)}, u32[]{:S(2)}, u32[]{:S(2)}) collective-permute-start(f32[56,128]{1,0:T(8,128)S(1)} %get-tuple-element.25.refs_0_), channel_id=1, source_target_pairs={{0,1},{1,0},{2,3},{3,2},{4,5},{5,4},{6,7},{7,6},{8,9},{9,8},{10,11... | collective-permute-start | bytes 86024 | tf_op jit(solution)/shard_map/ppermute | solution.py:451
  15.4 2.1 %copy-start.1 = (f32[1,1,36,1024]{3,1,2,0:T(1,128)S(1)}, f32[1,1,36,1024]{3,1,2,0:T(1,128)}, u32[]{:S(2)}) copy-start(f32[1,1,36,1024]{3,1,2,0:T(1,128)} %param.19) | copy-start | bytes 442372
  15.4 2.1 %copy-start.4 = (f32[1,1,6,1024]{3,1,2,0:T(1,128)S(1)}, f32[1,1,6,1024]{3,1,2,0:T(1,128)}, u32[]{:S(2)}) copy-start(f32[1,1,6,1024]{3,1,2,0:T(1,128)} %param.25) | copy-start | bytes 73732

commit v8 on v7

--- a/solution.py
+++ b/solution.py
@@ -262,7 +262,7 @@
 
 def observe_kernel(
     copies_ref, measured_ref, jac_ref, slot_ref, pose_ref, duals_ref, live_ref, back_ref,
-    estimate_ref, out_ref, dual_ref, consensus_ref, planes_ref,
+    estimate_ref, self_ref, edge_ref, offset_ref, out_ref, dual_ref, consensus_ref, planes_ref,
 ):
     for v in range(3):
         consensus_ref[v] = estimate_ref[v]
@@ -289,14 +289,22 @@
         rows,
         out_rows,
     )
+    grad = []
     for a in range(6):
         high, middle, low = (
             sums[(s * 6 + a) * out_rows : (s * 6 + a + 1) * out_rows] for s in range(3)
         )
-        out_ref[a] = high + (middle + low)
-
-
-def refine_kernel(landmark_total, edge_ref, grad_ref, inverse_ref, offset_ref, *refs):
+        grad.append(high + (middle + low))
+    edge = edge_ref[...]
+    count = out_rows * LANES
+    tables = [[self_ref[a, pl.ds(k, 1), :] for k in range(out_rows)] for a in range(6)]
+    near = lookup(tables, lax.rem(edge, count), out_rows)
+    here = edge // count == lax.axis_index("sub")
+    for a in range(6):
+        out_ref[a] = grad[a] + jnp.where(here, near[a], 0.0) - self_ref[a] - offset_ref[a]
+
+
+def refine_kernel(landmark_total, edge_ref, grad_ref, inverse_ref, *refs):
     blocks, (out_ref, norm_ref) = refs[:-2], refs[-2:]
     subs = len(blocks)
     rows = edge_ref.shape[0]
@@ -305,12 +313,13 @@
     edge = edge_ref[...]
     place = lax.bitwise_xor(edge // count, me)
     tables = [
-        [held[pl.ds(a * rows + k, 1), :] for held in blocks for k in range(rows)]
+        [held[pl.ds(a * rows + k, 1), :] for held in blocks[1:] for k in range(rows)]
         for a in range(6)
     ]
-    far = lookup(tables, place * count + lax.rem(edge, count), rows)
+    far = lookup(tables, (place - 1) * count + lax.rem(edge, count), rows)
+    far = [jnp.where(place == 0, 0.0, value) for value in far]
     own = [blocks[0][pl.ds(a * rows, rows), :] for a in range(6)]
-    grad = [grad_ref[a] + far[a] - own[a] - offset_ref[a] for a in range(6)]
+    grad = [grad_ref[a] + far[a] for a in range(6)]
     for a in range(6):
         delta = inverse_ref[a * 6] * grad[0]
         for b in range(1, 6):
@@ -453,7 +462,7 @@
     grad_obs, dual_new, consensus = call(
         observe_kernel,
         [vmem(6, pose_rows, LANES), (3, rows, LANES), (3, owned_rows, LANES)],
-        [VMEM] * 9,
+        [VMEM] * 12,
         scratch=[pltpu.VMEM((18, obs_rows, LANES), jnp.float32)],
     )(
         in_vmem(copies),
@@ -465,18 +474,20 @@
         in_vmem(live),
         in_vmem(back),
         in_vmem(estimate),
+        in_vmem(pose_block),
+        in_vmem(edges),
+        in_vmem(offset),
     )
 
     refined, residual_norms = call(
         functools.partial(refine_kernel, float(owned * robots * subs)),
         [(6, pose_rows, LANES), (2,)],
-        [VMEM] * (4 + subs),
+        [VMEM] * (3 + subs),
         out_specs=[VMEM, SMEM],
     )(
         in_vmem(edges),
         in_vmem(grad_obs),
         in_vmem(inverse),
-        in_vmem(offset),
         *[in_vmem(value) for value in held],
     )
     return (

time: 18.7 us -> 18.6 us (level)
  no operation moved by 1% of the time
where the time goes in v8:
time: 18.6 us; the launch traced here: 18.4 us
  blocking collectives  11.3 us (61%)
  Pallas kernels  3.52 us (19%)
  starting transfers between devices  1.92 us (10%)
  waiting for transfers between devices  0.93 us (5%)
  between operations  0.71 us (4%)
    all_to_all x1, blocking collectives, over_robots(): lax.all_to_all(blocks, 'robot', 0, 0, tiled=True, axis_index_groups=groups)  11.3 us
    ppermute x3, starting transfers between devices, step(): held.append(lax.ppermute(sending, 'sub', ring))  1.92 us
    pallas_call x1, Pallas kernels, step(): call(observe_kernel, [vmem(6, pose_rows, LANES), (3, rows, LANES), (3, ow...  1.12 us
    ppermute x3, waiting for transfers between devices, step(): held.append(lax.ppermute(sending, 'sub', ring))  0.93 us
    pallas_call x1, Pallas kernels, step(): call(functools.partial(refine_kernel, float(owned * robots * subs)), [(6,...  0.89 us
    pallas_call x1, Pallas kernels, step(): call(functools.partial(pack_kernel, block), [vmem(robots * height, LANES)...  0.83 us
    pallas_call x1, Pallas kernels, step(): call(functools.partial(consensus_kernel, block, owned_rows, order), [vmem...  0.67 us
  transfers between devices with their start and end apart: 3, of which 2 were waited for; matrix products, arithmetic and copies ran while one was open for 0% of the time, Pallas kernels for 6%

profile of v8, /device:TPU:0, one launch (start us, length us, event | category | flops | bytes accessed | tf_op | source)
XLA Modules:
  0.0 18.4 jit_solution(14594132042254732036)
XLA Ops:
  0.6 0.0 copy-start
  0.6 0.8 %shard_map.156 = (f32[328,128]{1,0:T(8,128)S(1)}, f32[4,128]{1,0:T(4,128)S(1)}, f32[3,4,128]{2,1,0:T(4,128)S(1)}, f32[3,4,128]{2,1,0:T(4,128)S(1)}, s32[8,128]{1,0:T(8,128)S(1)}) custom-call(s32[1,8]{1,0:T(1,128)} %bitcast.33, f32[3,4,128]{2,1,0:T(4,128)} %bitcast.28, f32[3,4,128]{2,1,0:T(4,128)} %bitcast.29, s32[4,128]{1,0:T(4,128)} %bitcast.32, ...), custom_call_target="tpu_custom_call" | custom-call | tf_op jit(solution)/shard_map/pallas_call | solution.py:424
  1.5 0.0 copy-start.2
  1.5 11.3 %all_to_all.5 = f32[8,1,5248]{2,1,0:T(1,128)S(1)} all-to-all(f32[8,1,5248]{2,1,0:T(1,128)S(1)} %bitcast.20), channel_id=1, replica_groups={{20,12,0,28,24,8,4,16},{21,13,1,29,25,9,5,17},{22,14,2,30,26,10,6,18},{..., dimensions={0} | all-to-all | bytes 335872 | tf_op jit(solution)/shard_map/all_to_all | solution.py:360
  12.8 0.0 copy-done.2
  12.8 0.0 copy-start.3
  12.8 0.0 copy-start.4
  12.8 0.0 copy-start.6
  12.8 0.7 %shard_map.157 = (f32[56,128]{1,0:T(8,128)S(1)}, f32[3,4,128]{2,1,0:T(4,128)S(1)}, f32[3,4,128]{2,1,0:T(4,128)S(1)}) custom-call(f32[328,128]{1,0:T(8,128)S(1)} %bitcast.18, f32[6,8,128]{2,1,0:T(8,128)S(1)} %bitcast.22), custom_call_target="tpu_custom_call" | custom-call | tf_op jit(solution)/shard_map/pallas_call | solution.py:433
  13.5 0.0 copy-start.5
  13.5 0.1 collective-permute-start.2
  13.6 1.6 %collective-permute-start.1 = (f32[56,128]{1,0:T(8,128)S(1)}, f32[56,128]{1,0:T(8,128)S(1)}, u32[]{:S(2)}, u32[]{:S(2)}) collective-permute-start(f32[56,128]{1,0:T(8,128)S(1)} %get-tuple-element.25.refs_0_), channel_id=1, source_target_pairs={{0,2},{1,3},{2,0},{3,1},{4,6},{5,7},{6,4},{7,5},{8,10},{9,11},{10,... | collective-permute-start | bytes 86024 | tf_op jit(solution)/shard_map/ppermute | solution.py:460
  15.2 0.3 %collective-permute-start = (f32[56,128]{1,0:T(8,128)S(1)}, f32[56,128]{1,0:T(8,128)S(1)}, u32[]{:S(2)}, u32[]{:S(2)}) collective-permute-start(f32[56,128]{1,0:T(8,128)S(1)} %get-tuple-element.25.refs_0_), channel_id=1, source_target_pairs={{0,1},{1,0},{2,3},{3,2},{4,5},{5,4},{6,7},{7,6},{8,9},{9,8},{10,11... | collective-permute-start | bytes 86024 | tf_op jit(solution)/shard_map/ppermute | solution.py:460
  15.4 0.0 copy-done
  15.4 0.0 copy-done.3
  15.4 0.0 copy-done.4
  15.4 0.0 copy-done.6
  15.4 0.0 copy-done.5
  15.4 0.0 copy-start.1
  15.5 1.1 %shard_map.158 = (f32[6,8,128]{2,1,0:T(8,128)S(1)}, f32[3,4,128]{2,1,0:T(4,128)}, f32[3,4,128]{2,1,0:T(4,128)}) custom-call(f32[3,4,128]{2,1,0:T(4,128)S(1)} %get-tuple-element.18.copies_ref, f32[3,32,128]{2,1,0:T(8,128)S(1)} %bitcast.24, f32[18,32,128]{2,1,0:T(8,128)S(1)} %bitcast.19, s32[32,128]{1,0:T(8,128)S(1)} %bitcast.26, s32[32,128]{1,0:T(8,128)S(1)} %bitcast.27, ...), custom_call_target="tpu_custom_call" | custom-call | tf_op jit(solution)/shard_map/pallas_call | solution.py:462
  16.6 0.5 %collective-permute-done.2.refs_3_ = f32[56,128]{1,0:T(8,128)S(1)} collective-permute-done((f32[56,128]{1,0:T(8,128)S(1)}, f32[56,128]{1,0:T(8,128)S(1)}, u32[]{:S(2)}, u32[]{:S(2)}) %collective-permute-start.2) | collective-permute-done | bytes 28704 | tf_op jit(solution)/shard_map/ppermute | solution.py:460
  17.1 0.4 %collective-permute-done.1.refs_2_ = f32[56,128]{1,0:T(8,128)S(1)} collective-permute-done((f32[56,128]{1,0:T(8,128)S(1)}, f32[56,128]{1,0:T(8,128)S(1)}, u32[]{:S(2)}, u32[]{:S(2)}) %collective-permute-start.1) | collective-permute-done | bytes 28704 | tf_op jit(solution)/shard_map/ppermute | solution.py:460
  17.5 0.0 collective-permute-done.refs_1_
  17.5 0.0 copy-done.1
  17.5 0.9 %shard_map.159 = (f32[6,8,128]{2,1,0:T(8,128)}, f32[2]{0:T(128)}) custom-call(s32[8,128]{1,0:T(8,128)S(1)} %get-tuple-element.17.edge_ref, f32[6,8,128]{2,1,0:T(8,128)S(1)} %get-tuple-element.24.grad_ref, f32[36,8,128]{2,1,0:T(8,128)S(1)} %bitcast.21, f32[56,128]{1,0:T(8,128)S(1)} %get-tuple-element.25.refs_0_, f32[56,128]{1,0:T(8,128)S(1)} %collective-permute-done.refs_1_, ...), custom_call_target="tpu_custom_call" | custom-call | tf_op jit(solution)/shard_map/pallas_call | solution.py:482
Async XLA Ops:
  0.6 14.8 %copy-start = (f32[1,1,18,4096]{3,1,2,0:T(1,128)S(1)}, f32[1,1,18,4096]{3,1,2,0:T(1,128)}, u32[]{:S(2)}) copy-start(f32[1,1,18,4096]{3,1,2,0:T(1,128)} %param.20) | copy-start | bytes 884740
  1.5 11.3 %copy-start.2 = (f32[1,1,6,1024]{3,1,2,0:T(1,128)S(1)}, f32[1,1,6,1024]{3,1,2,0:T(1,128)}, u32[]{:S(2)}) copy-start(f32[1,1,6,1024]{3,1,2,0:T(1,128)} %param.18) | copy-start | bytes 73732
  12.8 2.6 %copy-start.3 = (f32[1,1,3,4096]{3,1,2,0:T(1,128)S(1)}, f32[1,1,3,4096]{3,1,2,0:T(1,128)}, u32[]{:S(2)}) copy-start(f32[1,1,3,4096]{3,1,2,0:T(1,128)} %param.21) | copy-start | bytes 147460
  12.8 2.6 %copy-start.4 = (f32[1,1,6,1024]{3,1,2,0:T(1,128)S(1)}, f32[1,1,6,1024]{3,1,2,0:T(1,128)}, u32[]{:S(2)}) copy-start(f32[1,1,6,1024]{3,1,2,0:T(1,128)} %param.25) | copy-start | bytes 73732
  12.8 2.6 %copy-start.6 = (s32[1,1,4096]{2,1,0:T(1,128)S(1)}, s32[1,1,4096]{2,1,0:T(1,128)}, u32[]{:S(2)}) copy-start(s32[1,1,4096]{2,1,0:T(1,128)} %param.22) | copy-start | bytes 49156
  13.5 2.0 %copy-start.5 = (s32[1,1,4096]{2,1,0:T(1,128)S(1)}, s32[1,1,4096]{2,1,0:T(1,128)}, u32[]{:S(2)}) copy-start(s32[1,1,4096]{2,1,0:T(1,128)} %param.23) | copy-start | bytes 49156
  13.5 3.6 %collective-permute-start.2 = (f32[56,128]{1,0:T(8,128)S(1)}, f32[56,128]{1,0:T(8,128)S(1)}, u32[]{:S(2)}, u32[]{:S(2)}) collective-permute-start(f32[56,128]{1,0:T(8,128)S(1)} %get-tuple-element.25.refs_0_), channel_id=1, source_target_pairs={{0,3},{1,2},{2,1},{3,0},{4,7},{5,6},{6,5},{7,4},{8,11},{9,10},{10,... | collective-permute-start | bytes 86024 | tf_op jit(solution)/shard_map/ppermute | solution.py:460
  13.6 3.9 %collective-permute-start.1 = (f32[56,128]{1,0:T(8,128)S(1)}, f32[56,128]{1,0:T(8,128)S(1)}, u32[]{:S(2)}, u32[]{:S(2)}) collective-permute-start(f32[56,128]{1,0:T(8,128)S(1)} %get-tuple-element.25.refs_0_), channel_id=1, source_target_pairs={{0,2},{1,3},{2,0},{3,1},{4,6},{5,7},{6,4},{7,5},{8,10},{9,11},{10,... | collective-permute-start | bytes 86024 | tf_op jit(solution)/shard_map/ppermute | solution.py:460
  15.2 2.4 %collective-permute-start = (f32[56,128]{1,0:T(8,128)S(1)}, f32[56,128]{1,0:T(8,128)S(1)}, u32[]{:S(2)}, u32[]{:S(2)}) collective-permute-start(f32[56,128]{1,0:T(8,128)S(1)} %get-tuple-element.25.refs_0_), channel_id=1, source_target_pairs={{0,1},{1,0},{2,3},{3,2},{4,5},{5,4},{6,7},{7,6},{8,9},{9,8},{10,11... | collective-permute-start | bytes 86024 | tf_op jit(solution)/shard_map/ppermute | solution.py:460
  15.4 2.1 %copy-start.1 = (f32[1,1,36,1024]{3,1,2,0:T(1,128)S(1)}, f32[1,1,36,1024]{3,1,2,0:T(1,128)}, u32[]{:S(2)}) copy-start(f32[1,1,36,1024]{3,1,2,0:T(1,128)} %param.19) | copy-start | bytes 442372
